TPU v7x, 256 devices: a whole 4x4x8 slice. The times are simulated.
256 devices in a mesh: tm: 64 (over z, y_lo, x), space: 4 (over y_hi, core).
Axes of the slice: x: 4, y: 4 (y_hi: 2, y_lo: 2; y = y_hi * 2 + y_lo), z: 8, core: 2. Of those that a mesh axis runs over, the one named last changes fastest.
Arguments:
- checkpoint: float32 [64, 4, 64, 1024], P('tm', None, 'space'), may hold values from -6 to 6
- advect: float32 [64, 2, 64, 1024], P('tm', None, 'space'), may hold values from -0.2 to 0.2
- diffuse: float32 [64, 64, 1024], P('tm', 'space'), may hold values from 0.1 to 0.2
- obs_rows: int32 [64, 8, 8], P('tm', None, 'space'), may hold values from 0 to 1
- obs_values: float32 [64, 8, 8, 4, 8, 1024], P('tm', None, 'space'), may hold values from -6 to 6
- obs_weight: float32 [64], P('tm'), may hold values from 0.5 to 13.5
- error_inverse: float32 [64, 4], P('tm'), may hold values from 0.3 to 3
- rates: float32 [64, 4], replicated, may hold values from 0.3971641 to 1, as said below
Outputs:
- direction: float32 [64, 4, 64, 1024], P('tm', None, 'space')
- grad_rms: float32 [], replicated
Inputs may be any that keep to these rules, and one draw needn't show every extreme that they name: `obs_rows`: entry i of the last dimension counts blocks of 8 rows within the rows of space block i // 2; repeats may occur. `rates`: every entry is below 1.
All inputs are finite; a program needn't handle non-finite values.
Results may differ from a plain program's by a relative error of at most 0.0003.
Values sent between devices are 32-bit elements; how exact they have to be, the bound alone decides.
No kernel may reach another device: no remote copies, remote signals or barrier semaphores. Data moves between devices by JAX's collectives and lax.ppermute only.
A program may use at most 64 MiB of HBM per device.

v0:
```python
import functools

import jax
import jax.numpy as jnp
from jax import lax
from jax.sharding import Mesh
from jax.sharding import PartitionSpec as P

STEPS = 8
BLOCK = 8
SPACE = ("space_0", "space_1")
TM = ("tm_0", "tm_1", "tm_2")
TM_SPACE = ("tm_0", "tm_1", "tm_2", "space_0", "space_1")


def padded_2(block, sides, width):
    for axis, dim in sides:
        count = lax.axis_size(axis)
        forward = [(i, i + 1) for i in range(count - 1)]
        backward = [(target, source) for source, target in forward]
        low = lax.ppermute(
            lax.slice_in_dim(block, block.shape[dim] - width, None, axis=dim), axis, forward
        )
        high = lax.ppermute(lax.slice_in_dim(block, 0, width, axis=dim), axis, backward)
        block = jnp.concatenate([low, block, high], axis=dim)
    return block


def passed_along(value, axis, steps):
    count = lax.axis_size(axis)
    leading, last = (max(0, -steps), min(count, count - steps))
    return lax.ppermute(value, axis, [(source, source + steps) for source in range(leading, last)])


def one_axis_at_a_time(x, axes):
    return functools.reduce(lax.psum, axes, x)


def stencil_of(advect_one, diffuse_one):
    centre = 1.0 - 4.0 * diffuse_one
    to_east = diffuse_one - 0.5 * advect_one[0]
    to_west = diffuse_one + 0.5 * advect_one[0]
    to_north = diffuse_one - 0.5 * advect_one[1]
    to_south = diffuse_one + 0.5 * advect_one[1]
    return (centre, to_east, to_west, to_north, to_south)


def advance(field_now, stencil):
    centre, to_east, to_west, to_north, to_south = stencil
    padded = padded_2(field_now, ((SPACE, 1),), 1)
    return (
        centre * field_now
        + to_east * jnp.roll(field_now, -1, axis=2)
        + to_west * jnp.roll(field_now, 1, axis=2)
        + to_north * padded[:, 2:]
        + to_south * padded[:, :-2]
    )


def retreat(costate, stencil, north_pad, south_pad):
    padded = padded_2(costate, ((SPACE, 1),), 1)
    centre, to_east, to_west = (stencil[0], stencil[1], stencil[2])
    return (
        centre * costate
        + jnp.roll(to_east * costate, 1, axis=2)
        + jnp.roll(to_west * costate, -1, axis=2)
        + (north_pad * padded)[:, :-2]
        + (south_pad * padded)[:, 2:]
    )


def select_rows(field_now, picker):
    blocks = field_now.reshape(field_now.shape[0], picker.shape[1], BLOCK, field_now.shape[2])
    return jnp.einsum("kb,cbrx->kcrx", picker, blocks, precision=lax.Precision.HIGHEST)


def spread_rows(misfit, picker, field_shape):
    placed = jnp.einsum("kb,kcrx->cbrx", picker, misfit, precision=lax.Precision.HIGHEST)
    return placed.reshape(field_shape)


def weigh_own(field_now, initial, inverse_row):
    prior_end = passed_along(field_now, TM, 1)
    return inverse_row[:, None, None] * (initial - prior_end)


def adjoint_sweep(misfits, pickers, weight, later_term, stencil, north_pad, south_pad, field_shape):
    costate = spread_rows(weight * misfits[STEPS - 1], pickers[STEPS - 1], field_shape) - later_term
    for moment in range(STEPS, 0, -1):
        costate = retreat(costate, stencil, north_pad, south_pad)
        if moment >= 2:
            costate = costate + spread_rows(
                weight * misfits[moment - 2], pickers[moment - 2], field_shape
            )
    return costate


def combine(earlier, latter):
    return (earlier[0] * latter[0], latter[0] * earlier[1] + latter[1])


def on_device(checkpoint, advect, diffuse, obs_rows, obs_values, obs_weight, error_inverse, rates):
    initial = checkpoint[0]
    field_shape = initial.shape
    next_start, next_inverse = passed_along((initial, error_inverse[0]), TM, -1)
    stencil = stencil_of(advect[0], diffuse[0])
    rim_coefs = padded_2(jnp.stack([advect[0, 1], diffuse[0]]), ((SPACE, 1),), 1)
    north_pad = rim_coefs[1] - 0.5 * rim_coefs[0]
    south_pad = rim_coefs[1] + 0.5 * rim_coefs[0]
    block_count = field_shape[1] // BLOCK
    block_ids = jnp.arange(block_count, dtype=jnp.int32)
    pickers = [
        (obs_rows[0, moment][:, None] == block_ids[None, :]).astype(jnp.float32)
        for moment in range(STEPS)
    ]
    field_now = initial
    misfits = []
    for moment in range(STEPS):
        field_now = advance(field_now, stencil)
        misfits.append(select_rows(field_now, pickers[moment]) - obs_values[0, moment])
    weight = obs_weight[0]
    later_term = next_inverse[:, None, None] * (next_start - field_now)
    costate = adjoint_sweep(
        misfits, pickers, weight, later_term, stencil, north_pad, south_pad, field_shape
    )
    weighted = weigh_own(field_now, initial, error_inverse[0])
    gradient = costate + weighted
    square_sum = one_axis_at_a_time(jnp.sum(gradient * gradient), TM_SPACE)
    entries = lax.axis_size(TM) * lax.axis_size(SPACE) * gradient.size
    rms_value = jnp.sqrt(square_sum / entries + 1e-06)
    position = lax.axis_index(TM)
    windows = lax.axis_size(TM)
    innovation = jnp.sqrt(1.0 - rates * rates)
    next_rates = jnp.concatenate([rates[1:], jnp.zeros((1, rates.shape[1]), jnp.float32)], axis=0)
    column_count = gradient.size // windows
    flat_grad = gradient.reshape(1, gradient.size)
    columns = lax.all_to_all(flat_grad, TM, split_axis=1, concat_axis=0, tiled=True)
    places = position * column_count + jnp.arange(column_count, dtype=jnp.int32)
    member = places // (field_shape[1] * field_shape[2])
    onehot = (member[None, :] == jnp.arange(field_shape[0], dtype=jnp.int32)[:, None]).astype(
        jnp.float32
    )
    rate_cols = jnp.dot(rates, onehot, precision=lax.Precision.HIGHEST)
    inno_cols = jnp.dot(innovation, onehot, precision=lax.Precision.HIGHEST)
    next_cols = jnp.dot(next_rates, onehot, precision=lax.Precision.HIGHEST)
    forward_cols = lax.associative_scan(combine, (rate_cols, inno_cols * columns), axis=0)[1]
    backward_cols = lax.associative_scan(
        combine, (next_cols, inno_cols * forward_cols), reverse=True, axis=0
    )[1]
    flat_back = lax.all_to_all(backward_cols, TM, split_axis=0, concat_axis=1, tiled=True)
    smoothed = flat_back.reshape(field_shape)
    direction = (smoothed / rms_value)[None]
    return (direction, rms_value)


def solution(mesh):
    torus = Mesh(
        mesh.devices.reshape(8, 2, 4, 2, 2), ("tm_0", "tm_1", "tm_2", "space_0", "space_1")
    )
    return jax.shard_map(
        on_device,
        mesh=torus,
        in_specs=(
            P(TM, None, SPACE, None),
            P(TM, None, SPACE, None),
            P(TM, SPACE, None),
            P(TM, None, SPACE),
            P(TM, None, SPACE, None, None, None),
            P(TM),
            P(TM, None),
            P(),
        ),
        out_specs=(P(TM, None, SPACE, None), P()),
        check_vma=False,
    )
```

profile of v0, /device:TPU:1, one launch (start us, length us, event | category | flops | bytes accessed | tf_op | source)
XLA Modules:
  0.0 256.4 jit_solution(6133454303341708587)
XLA Ops:
  2.9 6.2 %collective-permute-start.1 = (f32[4,1,1024]{2,1,0:T(1,128)S(1)}, f32[4,1,1024]{2,1,0:T(1,128)S(1)}, u32[]{:S(2)}, u32[]{:S(2)}) collective-permute-start(f32[4,1,1024]{2,1,0:T(1,128)S(1)} %get-tuple-element.101), channel_id=1, source_target_pairs={{0,1},{1,2},{2,3},{4,5},{5,6},{6,7},{8,9},{9,10},{10,11},{12,13},{... | collective-permute-start | bytes 49160 | tf_op jit(solution)/shard_map/ppermute | solution.py:21
  14.6 5.1 %collective-permute-start.18 = (f32[2,1,1024]{2,1,0:T(1,128)S(1)}, f32[2,1,1024]{2,1,0:T(1,128)S(1)}, u32[]{:S(2)}, u32[]{:S(2)}) collective-permute-start(f32[2,1,1024]{2,1,0:T(1,128)S(1)} %get-tuple-element.112), channel_id=1, source_target_pairs={{0,1},{1,2},{2,3},{4,5},{5,6},{6,7},{8,9},{9,10},{10,11},{12,13},{... | collective-permute-start | bytes 24584 | tf_op jit(solution)/shard_map/ppermute | solution.py:21
  22.8 2.4 fusion.167
  28.0 2.4 collective-permute-start.3
  34.0 3.0 %collective-permute-done.2 = f32[4,1,1024]{2,1,0:T(1,128)S(1)} collective-permute-done((f32[4,1,1024]{2,1,0:T(1,128)S(1)}, f32[4,1,1024]{2,1,0:T(1,128)S(1)}, u32[]{:S(2)}, u32[]{:S(2)}) %collective-permute-start.2) | collective-permute-done | bytes 16416 | tf_op jit(solution)/shard_map/ppermute | solution.py:24
  37.4 2.2 collective-permute-start.5
  43.3 2.8 %collective-permute-done.4 = f32[4,1,1024]{2,1,0:T(1,128)S(1)} collective-permute-done((f32[4,1,1024]{2,1,0:T(1,128)S(1)}, f32[4,1,1024]{2,1,0:T(1,128)S(1)}, u32[]{:S(2)}, u32[]{:S(2)}) %collective-permute-start.4) | collective-permute-done | bytes 16416 | tf_op jit(solution)/shard_map/ppermute | solution.py:24
  52.4 2.8 %collective-permute-done.6 = f32[4,1,1024]{2,1,0:T(1,128)S(1)} collective-permute-done((f32[4,1,1024]{2,1,0:T(1,128)S(1)}, f32[4,1,1024]{2,1,0:T(1,128)S(1)}, u32[]{:S(2)}, u32[]{:S(2)}) %collective-permute-start.6) | collective-permute-done | bytes 16416 | tf_op jit(solution)/shard_map/ppermute | solution.py:24
  61.5 2.8 %collective-permute-done.8 = f32[4,1,1024]{2,1,0:T(1,128)S(1)} collective-permute-done((f32[4,1,1024]{2,1,0:T(1,128)S(1)}, f32[4,1,1024]{2,1,0:T(1,128)S(1)}, u32[]{:S(2)}, u32[]{:S(2)}) %collective-permute-start.8) | collective-permute-done | bytes 16416 | tf_op jit(solution)/shard_map/ppermute | solution.py:24
  64.6 2.2 collective-permute-start.11
  70.6 2.8 %collective-permute-done.10 = f32[4,1,1024]{2,1,0:T(1,128)S(1)} collective-permute-done((f32[4,1,1024]{2,1,0:T(1,128)S(1)}, f32[4,1,1024]{2,1,0:T(1,128)S(1)}, u32[]{:S(2)}, u32[]{:S(2)}) %collective-permute-start.10) | collective-permute-done | bytes 16416 | tf_op jit(solution)/shard_map/ppermute | solution.py:24
  75.9 2.3 collective-permute-start.12
  79.9 2.6 %collective-permute-done.12 = f32[4,1,1024]{2,1,0:T(1,128)S(1)} collective-permute-done((f32[4,1,1024]{2,1,0:T(1,128)S(1)}, f32[4,1,1024]{2,1,0:T(1,128)S(1)}, u32[]{:S(2)}, u32[]{:S(2)}) %collective-permute-start.12) | collective-permute-done | bytes 16416 | tf_op jit(solution)/shard_map/ppermute | solution.py:24
  82.8 2.4 collective-permute-start.15
  88.8 2.9 %collective-permute-done.14 = f32[4,1,1024]{2,1,0:T(1,128)S(1)} collective-permute-done((f32[4,1,1024]{2,1,0:T(1,128)S(1)}, f32[4,1,1024]{2,1,0:T(1,128)S(1)}, u32[]{:S(2)}, u32[]{:S(2)}) %collective-permute-start.14) | collective-permute-done | bytes 16416 | tf_op jit(solution)/shard_map/ppermute | solution.py:24
  91.9 4.9 %collective-permute-start.36 = (f32[4,16,1024]{2,1,0:T(8,128)S(1)}, f32[4,16,1024]{2,1,0:T(8,128)S(1)}, u32[]{:S(2)}, u32[]{:S(2)}) collective-permute-start(f32[4,16,1024]{2,1,0:T(8,128)S(1)} %fusion.33), channel_id=1, source_target_pairs={{0,4},{4,8},{8,12},{12,16},{16,20},{20,24},{24,28},{28,32},{32,36}... | collective-permute-start | bytes 786440 | tf_op jit(solution)/shard_map/ppermute | solution.py:32
  100.6 5.1 %collective-permute-start.20 = (f32[4,1,1024]{2,1,0:T(1,128)S(1)}, f32[4,1,1024]{2,1,0:T(1,128)S(1)}, u32[]{:S(2)}, u32[]{:S(2)}) collective-permute-start(f32[4,1,1024]{2,1,0:T(1,128)S(1)} %get-tuple-element.52), channel_id=1, source_target_pairs={{0,1},{1,2},{2,3},{4,5},{5,6},{6,7},{8,9},{9,10},{10,11},{12,13},{... | collective-permute-start | bytes 49160 | tf_op jit(solution)/shard_map/ppermute | solution.py:21
  109.0 5.6 %collective-permute-start.22 = (f32[4,1,1024]{2,1,0:T(1,128)S(1)}, f32[4,1,1024]{2,1,0:T(1,128)S(1)}, u32[]{:S(2)}, u32[]{:S(2)}) collective-permute-start(f32[4,1,1024]{2,1,0:T(1,128)S(1)} %get-tuple-element.50), channel_id=1, source_target_pairs={{0,1},{1,2},{2,3},{4,5},{5,6},{6,7},{8,9},{9,10},{10,11},{12,13},{... | collective-permute-start | bytes 49160 | tf_op jit(solution)/shard_map/ppermute | solution.py:21
  117.7 5.7 %collective-permute-start.24 = (f32[4,1,1024]{2,1,0:T(1,128)S(1)}, f32[4,1,1024]{2,1,0:T(1,128)S(1)}, u32[]{:S(2)}, u32[]{:S(2)}) collective-permute-start(f32[4,1,1024]{2,1,0:T(1,128)S(1)} %get-tuple-element.48), channel_id=1, source_target_pairs={{0,1},{1,2},{2,3},{4,5},{5,6},{6,7},{8,9},{9,10},{10,11},{12,13},{... | collective-permute-start | bytes 49160 | tf_op jit(solution)/shard_map/ppermute | solution.py:21
  126.5 5.7 %collective-permute-start.26 = (f32[4,1,1024]{2,1,0:T(1,128)S(1)}, f32[4,1,1024]{2,1,0:T(1,128)S(1)}, u32[]{:S(2)}, u32[]{:S(2)}) collective-permute-start(f32[4,1,1024]{2,1,0:T(1,128)S(1)} %get-tuple-element.46), channel_id=1, source_target_pairs={{0,1},{1,2},{2,3},{4,5},{5,6},{6,7},{8,9},{9,10},{10,11},{12,13},{... | collective-permute-start | bytes 49160 | tf_op jit(solution)/shard_map/ppermute | solution.py:21
  135.3 5.7 %collective-permute-start.28 = (f32[4,1,1024]{2,1,0:T(1,128)S(1)}, f32[4,1,1024]{2,1,0:T(1,128)S(1)}, u32[]{:S(2)}, u32[]{:S(2)}) collective-permute-start(f32[4,1,1024]{2,1,0:T(1,128)S(1)} %get-tuple-element.44), channel_id=1, source_target_pairs={{0,1},{1,2},{2,3},{4,5},{5,6},{6,7},{8,9},{9,10},{10,11},{12,13},{... | collective-permute-start | bytes 49160 | tf_op jit(solution)/shard_map/ppermute | solution.py:21
  144.2 5.7 %collective-permute-start.30 = (f32[4,1,1024]{2,1,0:T(1,128)S(1)}, f32[4,1,1024]{2,1,0:T(1,128)S(1)}, u32[]{:S(2)}, u32[]{:S(2)}) collective-permute-start(f32[4,1,1024]{2,1,0:T(1,128)S(1)} %get-tuple-element.42), channel_id=1, source_target_pairs={{0,1},{1,2},{2,3},{4,5},{5,6},{6,7},{8,9},{9,10},{10,11},{12,13},{... | collective-permute-start | bytes 49160 | tf_op jit(solution)/shard_map/ppermute | solution.py:21
  153.0 5.7 %collective-permute-start.32 = (f32[4,1,1024]{2,1,0:T(1,128)S(1)}, f32[4,1,1024]{2,1,0:T(1,128)S(1)}, u32[]{:S(2)}, u32[]{:S(2)}) collective-permute-start(f32[4,1,1024]{2,1,0:T(1,128)S(1)} %get-tuple-element.40), channel_id=1, source_target_pairs={{0,1},{1,2},{2,3},{4,5},{5,6},{6,7},{8,9},{9,10},{10,11},{12,13},{... | collective-permute-start | bytes 49160 | tf_op jit(solution)/shard_map/ppermute | solution.py:21
  161.9 5.7 %collective-permute-start.34 = (f32[4,1,1024]{2,1,0:T(1,128)S(1)}, f32[4,1,1024]{2,1,0:T(1,128)S(1)}, u32[]{:S(2)}, u32[]{:S(2)}) collective-permute-start(f32[4,1,1024]{2,1,0:T(1,128)S(1)} %get-tuple-element.38), channel_id=1, source_target_pairs={{0,1},{1,2},{2,3},{4,5},{5,6},{6,7},{8,9},{9,10},{10,11},{12,13},{... | collective-permute-start | bytes 49160 | tf_op jit(solution)/shard_map/ppermute | solution.py:21
  170.3 16.1 %all-to-all-start = ((f32[1,64,1024]{2,0,1:T(1,128)}), f32[1,64,1024]{2,0,1:T(1,128)S(1)}, u32[]{:S(2)}, u32[]{:S(2)}) async-start(f32[1,64,1024]{2,0,1:T(1,128)} %copy.66), calls=%async_computation | async-start | bytes 524288 | tf_op jit(solution)/shard_map/all_to_all | solution.py:137
  188.1 9.1 %all-to-all-done = f32[1,64,1024]{2,0,1:T(1,128)S(1)} async-done(((f32[1,64,1024]{2,0,1:T(1,128)}), f32[1,64,1024]{2,0,1:T(1,128)S(1)}, u32[]{:S(2)}, u32[]{:S(2)}) %all-to-all-start) | async-done | bytes 262176 | tf_op jit(solution)/shard_map/all_to_all | solution.py:137
  202.5 4.6 %all-to-all-start.1 = ((f32[64,1,1024]{2,1,0:T(1,128)}), f32[64,1,1024]{2,1,0:T(1,128)S(1)}, u32[]{:S(2)}, u32[]{:S(2)}) async-start(f32[64,1,1024]{2,1,0:T(1,128)} %copy.67), calls=%async_computation.1 | async-start | bytes 524288 | tf_op jit(solution)/shard_map/all_to_all | solution.py:150
  207.2 15.5 %psum.35 = f32[]{:T(128)} all-reduce(f32[]{:T(128)} %get-tuple-element.12), channel_id=1, replica_groups=mesh['tm_0'=8,'tm_1'=2,'tm_2'=4,'space_0'=2,'space_1'=2] {'tm_0'}, use_global_device_ids=true, to_apply=%region_1.2 | all-reduce | flops 1 | bytes 8 | tf_op jit(solution)/shard_map/psum | solution.py:36
  222.7 4.4 %psum.36 = f32[]{:T(128)} all-reduce(f32[]{:T(128)} %psum.35), channel_id=1, replica_groups=mesh['tm_0'=8,'tm_1'=2,'tm_2'=4,'space_0'=2,'space_1'=2] {'tm_1'}, use_global_device_ids=true, to_apply=%region_2.3 | all-reduce | flops 1 | bytes 8 | tf_op jit(solution)/shard_map/psum | solution.py:36
  227.1 8.7 %psum.37 = f32[]{:T(128)} all-reduce(f32[]{:T(128)} %psum.36), channel_id=1, replica_groups=mesh['tm_0'=8,'tm_1'=2,'tm_2'=4,'space_0'=2,'space_1'=2] {'tm_2'}, use_global_device_ids=true, to_apply=%region_3.4 | all-reduce | flops 1 | bytes 8 | tf_op jit(solution)/shard_map/psum | solution.py:36
  235.8 5.9 %psum.38 = f32[]{:T(128)} all-reduce(f32[]{:T(128)} %psum.37), channel_id=1, replica_groups=mesh['tm_0'=8,'tm_1'=2,'tm_2'=4,'space_0'=2,'space_1'=2] {'space_0'}, use_global_device_ids=true, to_apply=%region_4.5 | all-reduce | flops 1 | bytes 8 | tf_op jit(solution)/shard_map/psum | solution.py:36
  241.7 12.1 %psum.39 = f32[]{:T(128)} all-reduce(f32[]{:T(128)} %psum.38), channel_id=1, replica_groups=mesh['tm_0'=8,'tm_1'=2,'tm_2'=4,'space_0'=2,'space_1'=2] {'space_1'}, use_global_device_ids=true, to_apply=%region_5.6 | all-reduce | flops 1 | bytes 8 | tf_op jit(solution)/shard_map/psum | solution.py:36
  (321 shorter events, 80.3 us)
Async XLA Ops:
  0.6 97.8 %collective-permute-start.17 = (f32[4,16,1024]{2,1,0:T(8,128)}, f32[4,16,1024]{2,1,0:T(8,128)S(1)}, u32[]{:S(2)}, u32[]{:S(2)}) collective-permute-start(f32[4,16,1024]{2,1,0:T(8,128)} %bitcast.210), channel_id=1, source_target_pairs={{4,0},{8,4},{12,8},{16,12},{20,16},{24,20},{28,24},{32,28},{36,32}... | collective-permute-start | bytes 786440 | tf_op jit(solution)/shard_map/ppermute | solution.py:32
  2.9 24.7 %collective-permute-start.1 = (f32[4,1,1024]{2,1,0:T(1,128)S(1)}, f32[4,1,1024]{2,1,0:T(1,128)S(1)}, u32[]{:S(2)}, u32[]{:S(2)}) collective-permute-start(f32[4,1,1024]{2,1,0:T(1,128)S(1)} %get-tuple-element.101), channel_id=1, source_target_pairs={{0,1},{1,2},{2,3},{4,5},{5,6},{6,7},{8,9},{9,10},{10,11},{12,13},{... | collective-permute-start | bytes 49160 | tf_op jit(solution)/shard_map/ppermute | solution.py:21
  9.1 18.5 %collective-permute-start = (f32[4,1,1024]{2,1,0:T(1,128)S(1)}, f32[4,1,1024]{2,1,0:T(1,128)S(1)}, u32[]{:S(2)}, u32[]{:S(2)}) collective-permute-start(f32[4,1,1024]{2,1,0:T(1,128)S(1)} %get-tuple-element.100), channel_id=1, source_target_pairs={{1,0},{2,1},{3,2},{5,4},{6,5},{7,6},{9,8},{10,9},{11,10},{13,12},{... | collective-permute-start | bytes 49160 | tf_op jit(solution)/shard_map/ppermute | solution.py:24
  12.7 13.5 %collective-permute-start.19 = (f32[2,1,1024]{2,1,0:T(1,128)S(1)}, f32[2,1,1024]{2,1,0:T(1,128)S(1)}, u32[]{:S(2)}, u32[]{:S(2)}) collective-permute-start(f32[2,1,1024]{2,1,0:T(1,128)S(1)} %get-tuple-element.113), channel_id=1, source_target_pairs={{1,0},{2,1},{3,2},{5,4},{6,5},{7,6},{9,8},{10,9},{11,10},{13,12},{... | collective-permute-start | bytes 24584 | tf_op jit(solution)/shard_map/ppermute | solution.py:24
  14.6 12.9 %collective-permute-start.18 = (f32[2,1,1024]{2,1,0:T(1,128)S(1)}, f32[2,1,1024]{2,1,0:T(1,128)S(1)}, u32[]{:S(2)}, u32[]{:S(2)}) collective-permute-start(f32[2,1,1024]{2,1,0:T(1,128)S(1)} %get-tuple-element.112), channel_id=1, source_target_pairs={{0,1},{1,2},{2,3},{4,5},{5,6},{6,7},{8,9},{9,10},{10,11},{12,13},{... | collective-permute-start | bytes 24584 | tf_op jit(solution)/shard_map/ppermute | solution.py:21
  26.2 72.2 %collective-permute-start.16 = (f32[4]{0:T(128)S(1)}, f32[4]{0:T(128)S(1)}, u32[]{:S(2)}, u32[]{:S(2)}) collective-permute-start(f32[4]{0:T(128)S(1)} %bitcast.235), channel_id=1, source_target_pairs={{4,0},{8,4},{12,8},{16,12},{20,16},{24,20},{28,24},{32,28},{36,32}... | collective-permute-start | bytes 56 | tf_op jit(solution)/shard_map/ppermute | solution.py:32
  30.4 6.6 %collective-permute-start.2 = (f32[4,1,1024]{2,1,0:T(1,128)S(1)}, f32[4,1,1024]{2,1,0:T(1,128)S(1)}, u32[]{:S(2)}, u32[]{:S(2)}) collective-permute-start(f32[4,1,1024]{2,1,0:T(1,128)S(1)} %get-tuple-element.94), channel_id=1, source_target_pairs={{1,0},{2,1},{3,2},{5,4},{6,5},{7,6},{9,8},{10,9},{11,10},{13,12},{... | collective-permute-start | bytes 49160 | tf_op jit(solution)/shard_map/ppermute | solution.py:24
  39.5 6.6 %collective-permute-start.4 = (f32[4,1,1024]{2,1,0:T(1,128)S(1)}, f32[4,1,1024]{2,1,0:T(1,128)S(1)}, u32[]{:S(2)}, u32[]{:S(2)}) collective-permute-start(f32[4,1,1024]{2,1,0:T(1,128)S(1)} %get-tuple-element.88), channel_id=1, source_target_pairs={{1,0},{2,1},{3,2},{5,4},{6,5},{7,6},{9,8},{10,9},{11,10},{13,12},{... | collective-permute-start | bytes 49160 | tf_op jit(solution)/shard_map/ppermute | solution.py:24
  48.6 6.6 %collective-permute-start.6 = (f32[4,1,1024]{2,1,0:T(1,128)S(1)}, f32[4,1,1024]{2,1,0:T(1,128)S(1)}, u32[]{:S(2)}, u32[]{:S(2)}) collective-permute-start(f32[4,1,1024]{2,1,0:T(1,128)S(1)} %get-tuple-element.82), channel_id=1, source_target_pairs={{1,0},{2,1},{3,2},{5,4},{6,5},{7,6},{9,8},{10,9},{11,10},{13,12},{... | collective-permute-start | bytes 49160 | tf_op jit(solution)/shard_map/ppermute | solution.py:24
  57.7 6.6 %collective-permute-start.8 = (f32[4,1,1024]{2,1,0:T(1,128)S(1)}, f32[4,1,1024]{2,1,0:T(1,128)S(1)}, u32[]{:S(2)}, u32[]{:S(2)}) collective-permute-start(f32[4,1,1024]{2,1,0:T(1,128)S(1)} %get-tuple-element.76), channel_id=1, source_target_pairs={{1,0},{2,1},{3,2},{5,4},{6,5},{7,6},{9,8},{10,9},{11,10},{13,12},{... | collective-permute-start | bytes 49160 | tf_op jit(solution)/shard_map/ppermute | solution.py:24
  66.8 6.6 %collective-permute-start.10 = (f32[4,1,1024]{2,1,0:T(1,128)S(1)}, f32[4,1,1024]{2,1,0:T(1,128)S(1)}, u32[]{:S(2)}, u32[]{:S(2)}) collective-permute-start(f32[4,1,1024]{2,1,0:T(1,128)S(1)} %get-tuple-element.70), channel_id=1, source_target_pairs={{1,0},{2,1},{3,2},{5,4},{6,5},{7,6},{9,8},{10,9},{11,10},{13,12},{... | collective-permute-start | bytes 49160 | tf_op jit(solution)/shard_map/ppermute | solution.py:24
  73.7 6.2 %collective-permute-start.13 = (f32[4,1,1024]{2,1,0:T(1,128)S(1)}, f32[4,1,1024]{2,1,0:T(1,128)S(1)}, u32[]{:S(2)}, u32[]{:S(2)}) collective-permute-start(f32[4,1,1024]{2,1,0:T(1,128)S(1)} %get-tuple-element.65), channel_id=1, source_target_pairs={{0,1},{1,2},{2,3},{4,5},{5,6},{6,7},{8,9},{9,10},{10,11},{12,13},{... | collective-permute-start | bytes 49160 | tf_op jit(solution)/shard_map/ppermute | solution.py:21
  75.9 6.6 %collective-permute-start.12 = (f32[4,1,1024]{2,1,0:T(1,128)S(1)}, f32[4,1,1024]{2,1,0:T(1,128)S(1)}, u32[]{:S(2)}, u32[]{:S(2)}) collective-permute-start(f32[4,1,1024]{2,1,0:T(1,128)S(1)} %get-tuple-element.64), channel_id=1, source_target_pairs={{1,0},{2,1},{3,2},{5,4},{6,5},{7,6},{9,8},{10,9},{11,10},{13,12},{... | collective-permute-start | bytes 49160 | tf_op jit(solution)/shard_map/ppermute | solution.py:24
  85.2 6.6 %collective-permute-start.14 = (f32[4,1,1024]{2,1,0:T(1,128)S(1)}, f32[4,1,1024]{2,1,0:T(1,128)S(1)}, u32[]{:S(2)}, u32[]{:S(2)}) collective-permute-start(f32[4,1,1024]{2,1,0:T(1,128)S(1)} %get-tuple-element.58), channel_id=1, source_target_pairs={{1,0},{2,1},{3,2},{5,4},{6,5},{7,6},{9,8},{10,9},{11,10},{13,12},{... | collective-permute-start | bytes 49160 | tf_op jit(solution)/shard_map/ppermute | solution.py:24
  91.9 76.6 %collective-permute-start.36 = (f32[4,16,1024]{2,1,0:T(8,128)S(1)}, f32[4,16,1024]{2,1,0:T(8,128)S(1)}, u32[]{:S(2)}, u32[]{:S(2)}) collective-permute-start(f32[4,16,1024]{2,1,0:T(8,128)S(1)} %fusion.33), channel_id=1, source_target_pairs={{0,4},{4,8},{8,12},{12,16},{16,20},{20,24},{24,28},{28,32},{32,36}... | collective-permute-start | bytes 786440 | tf_op jit(solution)/shard_map/ppermute | solution.py:32
  98.6 8.1 %collective-permute-start.21 = (f32[4,1,1024]{2,1,0:T(1,128)S(1)}, f32[4,1,1024]{2,1,0:T(1,128)S(1)}, u32[]{:S(2)}, u32[]{:S(2)}) collective-permute-start(f32[4,1,1024]{2,1,0:T(1,128)S(1)} %get-tuple-element.53), channel_id=1, source_target_pairs={{1,0},{2,1},{3,2},{5,4},{6,5},{7,6},{9,8},{10,9},{11,10},{13,12},{... | collective-permute-start | bytes 49160 | tf_op jit(solution)/shard_map/ppermute | solution.py:24
  107.0 7.8 %collective-permute-start.23 = (f32[4,1,1024]{2,1,0:T(1,128)S(1)}, f32[4,1,1024]{2,1,0:T(1,128)S(1)}, u32[]{:S(2)}, u32[]{:S(2)}) collective-permute-start(f32[4,1,1024]{2,1,0:T(1,128)S(1)} %get-tuple-element.51), channel_id=1, source_target_pairs={{1,0},{2,1},{3,2},{5,4},{6,5},{7,6},{9,8},{10,9},{11,10},{13,12},{... | collective-permute-start | bytes 49160 | tf_op jit(solution)/shard_map/ppermute | solution.py:24
  109.0 6.4 %collective-permute-start.22 = (f32[4,1,1024]{2,1,0:T(1,128)S(1)}, f32[4,1,1024]{2,1,0:T(1,128)S(1)}, u32[]{:S(2)}, u32[]{:S(2)}) collective-permute-start(f32[4,1,1024]{2,1,0:T(1,128)S(1)} %get-tuple-element.50), channel_id=1, source_target_pairs={{0,1},{1,2},{2,3},{4,5},{5,6},{6,7},{8,9},{9,10},{10,11},{12,13},{... | collective-permute-start | bytes 49160 | tf_op jit(solution)/shard_map/ppermute | solution.py:21
  115.7 7.9 %collective-permute-start.25 = (f32[4,1,1024]{2,1,0:T(1,128)S(1)}, f32[4,1,1024]{2,1,0:T(1,128)S(1)}, u32[]{:S(2)}, u32[]{:S(2)}) collective-permute-start(f32[4,1,1024]{2,1,0:T(1,128)S(1)} %get-tuple-element.49), channel_id=1, source_target_pairs={{1,0},{2,1},{3,2},{5,4},{6,5},{7,6},{9,8},{10,9},{11,10},{13,12},{... | collective-permute-start | bytes 49160 | tf_op jit(solution)/shard_map/ppermute | solution.py:24
  117.7 6.6 %collective-permute-start.24 = (f32[4,1,1024]{2,1,0:T(1,128)S(1)}, f32[4,1,1024]{2,1,0:T(1,128)S(1)}, u32[]{:S(2)}, u32[]{:S(2)}) collective-permute-start(f32[4,1,1024]{2,1,0:T(1,128)S(1)} %get-tuple-element.48), channel_id=1, source_target_pairs={{0,1},{1,2},{2,3},{4,5},{5,6},{6,7},{8,9},{9,10},{10,11},{12,13},{... | collective-permute-start | bytes 49160 | tf_op jit(solution)/shard_map/ppermute | solution.py:21
  124.6 7.9 %collective-permute-start.27 = (f32[4,1,1024]{2,1,0:T(1,128)S(1)}, f32[4,1,1024]{2,1,0:T(1,128)S(1)}, u32[]{:S(2)}, u32[]{:S(2)}) collective-permute-start(f32[4,1,1024]{2,1,0:T(1,128)S(1)} %get-tuple-element.47), channel_id=1, source_target_pairs={{1,0},{2,1},{3,2},{5,4},{6,5},{7,6},{9,8},{10,9},{11,10},{13,12},{... | collective-permute-start | bytes 49160 | tf_op jit(solution)/shard_map/ppermute | solution.py:24
  126.5 6.6 %collective-permute-start.26 = (f32[4,1,1024]{2,1,0:T(1,128)S(1)}, f32[4,1,1024]{2,1,0:T(1,128)S(1)}, u32[]{:S(2)}, u32[]{:S(2)}) collective-permute-start(f32[4,1,1024]{2,1,0:T(1,128)S(1)} %get-tuple-element.46), channel_id=1, source_target_pairs={{0,1},{1,2},{2,3},{4,5},{5,6},{6,7},{8,9},{9,10},{10,11},{12,13},{... | collective-permute-start | bytes 49160 | tf_op jit(solution)/shard_map/ppermute | solution.py:21
  133.4 7.9 %collective-permute-start.29 = (f32[4,1,1024]{2,1,0:T(1,128)S(1)}, f32[4,1,1024]{2,1,0:T(1,128)S(1)}, u32[]{:S(2)}, u32[]{:S(2)}) collective-permute-start(f32[4,1,1024]{2,1,0:T(1,128)S(1)} %get-tuple-element.45), channel_id=1, source_target_pairs={{1,0},{2,1},{3,2},{5,4},{6,5},{7,6},{9,8},{10,9},{11,10},{13,12},{... | collective-permute-start | bytes 49160 | tf_op jit(solution)/shard_map/ppermute | solution.py:24
  135.3 6.6 %collective-permute-start.28 = (f32[4,1,1024]{2,1,0:T(1,128)S(1)}, f32[4,1,1024]{2,1,0:T(1,128)S(1)}, u32[]{:S(2)}, u32[]{:S(2)}) collective-permute-start(f32[4,1,1024]{2,1,0:T(1,128)S(1)} %get-tuple-element.44), channel_id=1, source_target_pairs={{0,1},{1,2},{2,3},{4,5},{5,6},{6,7},{8,9},{9,10},{10,11},{12,13},{... | collective-permute-start | bytes 49160 | tf_op jit(solution)/shard_map/ppermute | solution.py:21
  142.3 7.9 %collective-permute-start.31 = (f32[4,1,1024]{2,1,0:T(1,128)S(1)}, f32[4,1,1024]{2,1,0:T(1,128)S(1)}, u32[]{:S(2)}, u32[]{:S(2)}) collective-permute-start(f32[4,1,1024]{2,1,0:T(1,128)S(1)} %get-tuple-element.43), channel_id=1, source_target_pairs={{1,0},{2,1},{3,2},{5,4},{6,5},{7,6},{9,8},{10,9},{11,10},{13,12},{... | collective-permute-start | bytes 49160 | tf_op jit(solution)/shard_map/ppermute | solution.py:24
  144.2 6.6 %collective-permute-start.30 = (f32[4,1,1024]{2,1,0:T(1,128)S(1)}, f32[4,1,1024]{2,1,0:T(1,128)S(1)}, u32[]{:S(2)}, u32[]{:S(2)}) collective-permute-start(f32[4,1,1024]{2,1,0:T(1,128)S(1)} %get-tuple-element.42), channel_id=1, source_target_pairs={{0,1},{1,2},{2,3},{4,5},{5,6},{6,7},{8,9},{9,10},{10,11},{12,13},{... | collective-permute-start | bytes 49160 | tf_op jit(solution)/shard_map/ppermute | solution.py:21
  151.1 7.9 %collective-permute-start.33 = (f32[4,1,1024]{2,1,0:T(1,128)S(1)}, f32[4,1,1024]{2,1,0:T(1,128)S(1)}, u32[]{:S(2)}, u32[]{:S(2)}) collective-permute-start(f32[4,1,1024]{2,1,0:T(1,128)S(1)} %get-tuple-element.41), channel_id=1, source_target_pairs={{1,0},{2,1},{3,2},{5,4},{6,5},{7,6},{9,8},{10,9},{11,10},{13,12},{... | collective-permute-start | bytes 49160 | tf_op jit(solution)/shard_map/ppermute | solution.py:24
  153.0 6.6 %collective-permute-start.32 = (f32[4,1,1024]{2,1,0:T(1,128)S(1)}, f32[4,1,1024]{2,1,0:T(1,128)S(1)}, u32[]{:S(2)}, u32[]{:S(2)}) collective-permute-start(f32[4,1,1024]{2,1,0:T(1,128)S(1)} %get-tuple-element.40), channel_id=1, source_target_pairs={{0,1},{1,2},{2,3},{4,5},{5,6},{6,7},{8,9},{9,10},{10,11},{12,13},{... | collective-permute-start | bytes 49160 | tf_op jit(solution)/shard_map/ppermute | solution.py:21
  159.9 7.9 %collective-permute-start.35 = (f32[4,1,1024]{2,1,0:T(1,128)S(1)}, f32[4,1,1024]{2,1,0:T(1,128)S(1)}, u32[]{:S(2)}, u32[]{:S(2)}) collective-permute-start(f32[4,1,1024]{2,1,0:T(1,128)S(1)} %get-tuple-element.39), channel_id=1, source_target_pairs={{1,0},{2,1},{3,2},{5,4},{6,5},{7,6},{9,8},{10,9},{11,10},{13,12},{... | collective-permute-start | bytes 49160 | tf_op jit(solution)/shard_map/ppermute | solution.py:24
  161.9 6.6 %collective-permute-start.34 = (f32[4,1,1024]{2,1,0:T(1,128)S(1)}, f32[4,1,1024]{2,1,0:T(1,128)S(1)}, u32[]{:S(2)}, u32[]{:S(2)}) collective-permute-start(f32[4,1,1024]{2,1,0:T(1,128)S(1)} %get-tuple-element.38), channel_id=1, source_target_pairs={{0,1},{1,2},{2,3},{4,5},{5,6},{6,7},{8,9},{9,10},{10,11},{12,13},{... | collective-permute-start | bytes 49160 | tf_op jit(solution)/shard_map/ppermute | solution.py:21
  170.3 26.9 %all-to-all-start = ((f32[1,64,1024]{2,0,1:T(1,128)}), f32[1,64,1024]{2,0,1:T(1,128)S(1)}, u32[]{:S(2)}, u32[]{:S(2)}) async-start(f32[1,64,1024]{2,0,1:T(1,128)} %copy.66), calls=%async_computation | async-start | bytes 524288 | tf_op jit(solution)/shard_map/all_to_all | solution.py:137
  202.5 51.9 %all-to-all-start.1 = ((f32[64,1,1024]{2,1,0:T(1,128)}), f32[64,1,1024]{2,1,0:T(1,128)S(1)}, u32[]{:S(2)}, u32[]{:S(2)}) async-start(f32[64,1,1024]{2,1,0:T(1,128)} %copy.67), calls=%async_computation.1 | async-start | bytes 524288 | tf_op jit(solution)/shard_map/all_to_all | solution.py:150
  (13 other events, 81.0 us)
where the time goes:
time: 258 us; the launch traced here: 256 us
  starting transfers between devices  134 us (52%)
  blocking collectives  46.6 us (18%)
  waiting for transfers between devices  33.5 us (13%)
  local copies, waits for them, and re-layouts  16.3 us (6%)
  matrix products  13.4 us (5%)
  other arithmetic  7.26 us (3%)
  between operations  5.02 us (2%)
    ppermute x17, starting transfers between devices, padded_2(): lax.ppermute(lax.slice_in_dim(block, block.shape[dim] - width, None, axis...  71.9 us
    psum x5, blocking collectives, one_axis_at_a_time(): return functools.reduce(lax.psum, axes, x)  46.6 us
    ppermute x17, starting transfers between devices, padded_2(): lax.ppermute(lax.slice_in_dim(block, 0, width, axis=dim), axis, backward)  34 us
    ppermute x17, waiting for transfers between devices, padded_2(): lax.ppermute(lax.slice_in_dim(block, 0, width, axis=dim), axis, backward)  20.3 us
    all_to_all x1, starting transfers between devices, on_device(): lax.all_to_all(flat_grad, TM, split_axis=1, concat_axis=0, tiled=True)  16.1 us
    all_to_all x1, waiting for transfers between devices, on_device(): lax.all_to_all(flat_grad, TM, split_axis=1, concat_axis=0, tiled=True)  9.09 us
    ppermute x3, starting transfers between devices, passed_along(): lax.ppermute(value, axis, [(source, source + steps) for source in range(l...  7.5 us
    dot_general x8, matrix products, select_rows(): jnp.einsum('kb,cbrx->kcrx', picker, blocks, precision=lax.Precision.HIGHEST)  7.44 us
  transfers between devices with their start and end apart: 39, of which 16 were waited for; matrix products, arithmetic and copies ran while one was open for 12% of the time, Pallas kernels for 0%

commit v1 on v0

v1 whole, which is shorter than its diff:
```python
import jax
import jax.numpy as jnp
from jax import lax
from jax.experimental import pallas as pl
from jax.experimental.pallas import tpu as pltpu
from jax.sharding import Mesh
from jax.sharding import PartitionSpec as P

STEPS = 8
BLOCK = 8
COMPS = 4
ROWS = 16
LANES = 128
GROUPS = 8
COLUMNS = GROUPS * LANES
TALL = 48
FIRST = 8
OWN = 16
CELLS = COMPS * GROUPS
SPACE = ("space_0", "space_1")
TM = ("tm_0", "tm_1", "tm_2")
VMEM = pl.BlockSpec(memory_space=pltpu.VMEM)
SMEM = pl.BlockSpec(memory_space=pltpu.SMEM)
ANY = pl.BlockSpec(memory_space=pl.ANY)


def shape(*dims):
    return jax.ShapeDtypeStruct(dims, jnp.float32)


def lanes(group):
    return slice(group * LANES, (group + 1) * LANES)


def passed_along(value, axis, steps):
    count = lax.axis_size(axis)
    leading, last = (max(0, -steps), min(count, count - steps))
    return lax.ppermute(value, axis, [(source, source + steps) for source in range(leading, last)])


def swapped(value, axis):
    return lax.ppermute(value, axis, [(0, 1), (1, 0)])


def eastern(tiles, lane):
    turned = [pltpu.roll(tile, LANES - 1, 1) for tile in tiles]
    return [
        jnp.where(lane == LANES - 1, turned[(g + 1) % GROUPS], turned[g]) for g in range(GROUPS)
    ]


def western(tiles, lane):
    turned = [pltpu.roll(tile, 1, 1) for tile in tiles]
    return [jnp.where(lane == 0, turned[g - 1], turned[g]) for g in range(GROUPS)]


def coefficient_tiles(advect, diffuse, low, high, tile, group):
    if tile in (1, 2):
        rows = slice((tile - 1) * 8, tile * 8)
        east_flow = advect[0, rows, lanes(group)]
        north_flow = advect[1, rows, lanes(group)]
        spread = diffuse[rows, lanes(group)]
    else:
        side = low if tile == 0 else high
        east_flow = side[32:40, lanes(group)]
        north_flow = side[40:48, lanes(group)]
        spread = side[48:56, lanes(group)]
    return (
        1.0 - 4.0 * spread,
        spread - 0.5 * east_flow,
        spread + 0.5 * east_flow,
        spread - 0.5 * north_flow,
        spread + 0.5 * north_flow,
    )


def lane_index():
    return lax.broadcasted_iota(jnp.int32, (8, LANES), 1)


def stencil_tile(source, tile, lane, centre, east, west, north, south, store):
    fields = [[source(k, g, 0) for g in range(GROUPS)] for k in range(COMPS)]
    to_east = [eastern(row, lane) for row in fields]
    to_west = [western(row, lane) for row in fields]
    for g in range(GROUPS):
        c, e, w, n, s = centre(g), east(g), west(g), north(g), south(g)
        for k in range(COMPS):
            store(
                k,
                g,
                c * fields[k][g]
                + e * to_east[k][g]
                + w * to_west[k][g]
                + n * source(k, g, 1)
                + s * source(k, g, -1),
            )


def forward_kernel(checkpoint, advect, diffuse, low, high, history, last, coefs, work):
    lane = lane_index()
    nothing = jnp.zeros((8, LANES), jnp.float32)
    for g in range(GROUPS):
        for tile in range(4):
            rows = slice(FIRST + 8 * tile, FIRST + 8 * tile + 8)
            values = coefficient_tiles(advect, diffuse, low, high, tile, g)
            for which in range(5):
                coefs[which, g, rows, :] = values[which]
            for k in range(COMPS):
                if tile in (1, 2):
                    value = checkpoint[k, (tile - 1) * 8 : tile * 8, lanes(g)]
                else:
                    value = (low if tile == 0 else high)[8 * k : 8 * k + 8, lanes(g)]
                work[0, k * GROUPS + g, rows, :] = value
        for k in range(COMPS):
            for slot in range(2):
                work[slot, k * GROUPS + g, 0:8, :] = nothing
                work[slot, k * GROUPS + g, TALL - 8 : TALL, :] = nothing

    def step(moment, carry):
        now = lax.rem(moment, 2)
        after = 1 - now
        for tile in range(4):
            start = FIRST + 8 * tile

            def source(k, g, shift):
                return work[now, k * GROUPS + g, start + shift : start + shift + 8, :]

            def store(k, g, value):
                work[after, k * GROUPS + g, start : start + 8, :] = value
                if tile in (1, 2):
                    history[moment, k * GROUPS + g, (tile - 1) * 8 : tile * 8, :] = value

            loads = [
                lambda g, which=which: coefs[which, g, start : start + 8, :] for which in range(5)
            ]
            stencil_tile(source, tile, lane, *loads, store)
        return carry

    lax.fori_loop(0, STEPS, step, 0)
    for cell in range(CELLS):
        last[cell] = history[STEPS - 1, cell]


def adjoint_kernel(
    obs_rows, weight, advect, diffuse, low, high, history, following, obs_values,
    own, to_low, to_high, coefs, work, observed, arrivals,
):
    copies = [
        pltpu.make_async_copy(obs_values.at[moment], observed.at[moment], arrivals.at[moment])
        for moment in range(STEPS)
    ]
    for moment in reversed(range(STEPS)):
        copies[moment].start()
    lane = lane_index()
    nothing = jnp.zeros((8, LANES), jnp.float32)
    for tile in range(4):
        rows = slice(FIRST + 8 * tile, FIRST + 8 * tile + 8)
        groups = [
            coefficient_tiles(advect, diffuse, low, high, tile, g) for g in range(GROUPS)
        ]
        from_east = eastern([values[2] for values in groups], lane)
        from_west = western([values[1] for values in groups], lane)
        for g in range(GROUPS):
            coefs[0, g, rows, :] = groups[g][0]
            coefs[1, g, rows, :] = from_east[g]
            coefs[2, g, rows, :] = from_west[g]
            coefs[3, g, rows, :] = groups[g][4]
            coefs[4, g, rows, :] = groups[g][3]
    for g in range(GROUPS):
        for which in (3, 4):
            coefs[which, g, 0:8, :] = nothing
            coefs[which, g, TALL - 8 : TALL, :] = nothing
        for k in range(COMPS):
            cell = k * GROUPS + g
            for slot in range(2):
                work[slot, cell, 0:8, :] = nothing
                work[slot, cell, TALL - 8 : TALL, :] = nothing
            work[0, cell, 8:16, :] = nothing
            work[0, cell, 32:40, :] = nothing
            inverse = jnp.broadcast_to(following[64 + k : 65 + k, lanes(g)], (8, LANES))
            for half in range(2):
                start = following[16 * k + 8 * half : 16 * k + 8 * half + 8, lanes(g)]
                end = history[STEPS - 1, cell, 8 * half : 8 * half + 8, :]
                work[0, cell, OWN + 8 * half : OWN + 8 * half + 8, :] = inverse * (end - start)
    scale = weight[0]

    def step(turn, carry):
        moment = STEPS - 1 - turn
        now = lax.rem(turn, 2)
        after = 1 - now
        pltpu.make_async_copy(
            obs_values.at[moment], observed.at[moment], arrivals.at[moment]
        ).wait()
        for entry in range(2):
            offset = pl.multiple_of(obs_rows[moment, entry] * BLOCK, BLOCK)
            for k in range(COMPS):
                for g in range(GROUPS):
                    cell = k * GROUPS + g
                    misfit = (
                        history[moment, cell, pl.ds(offset, 8), :]
                        - observed[moment, entry, k, :, lanes(g)]
                    )
                    there = pl.ds(OWN + offset, 8)
                    work[now, cell, there, :] = work[now, cell, there, :] + scale * misfit
        for tile in range(4):
            start = FIRST + 8 * tile

            def source(k, g, shift):
                return work[now, k * GROUPS + g, start + shift : start + shift + 8, :]

            def store(k, g, value):
                work[after, k * GROUPS + g, start : start + 8, :] = value

            shifts = (0, 0, 0, 1, -1)
            loads = [
                lambda g, which=which: coefs[
                    which, g, start + shifts[which] : start + shifts[which] + 8, :
                ]
                for which in range(5)
            ]
            stencil_tile(source, tile, lane, *loads, store)
        return carry

    lax.fori_loop(0, STEPS, step, 0)
    for cell in range(CELLS):
        to_low[cell] = work[0, cell, 8:16, :]
        own[cell] = work[0, cell, 16:32, :]
        to_high[cell] = work[0, cell, 32:40, :]


def gradient_kernel(inverse, own, from_low, from_high, checkpoint, prior_end, parcels):
    squares = jnp.zeros((8, LANES), jnp.float32)
    for k in range(COMPS):
        scale = inverse[0, k]
        for g in range(GROUPS):
            cell = k * GROUPS + g
            for half in range(2):
                rows = slice(8 * half, 8 * half + 8)
                other = (from_low if half == 0 else from_high)[cell]
                forcing = checkpoint[k, rows, lanes(g)] - prior_end[cell, rows, :]
                value = own[cell, rows, :] + other + scale * forcing
                place = 9 * (2 * cell + half)
                parcels[place : place + 8, :] = value
                squares = squares + value * value
    total = jnp.sum(squares, axis=0, keepdims=True)
    for parcel in range(2 * CELLS):
        parcels[9 * parcel + 8 : 9 * parcel + 9, :] = total


def smoothing_kernel(component, rates, parcels, back, total):
    windows = back.shape[0]
    which = component[0]
    running = jnp.zeros((8, LANES), jnp.float32)
    sums = jnp.zeros((1, LANES), jnp.float32)
    kept = []
    for j in range(windows):
        rate = jnp.full((8, LANES), rates[j, which], jnp.float32)
        innovation = jnp.sqrt(1.0 - rate * rate)
        running = rate * running + innovation * parcels[9 * j : 9 * j + 8, :]
        back[j] = innovation * running
        sums = sums + parcels[9 * j + 8 : 9 * j + 9, :]
    total[...] = sums
    running = back[windows - 1]
    for j in range(windows - 2, -1, -1):
        rate = jnp.full((8, LANES), rates[j + 1, which], jnp.float32)
        running = back[j] + rate * running
        back[j] = running


def final_kernel(entries, back, total, direction, rms):
    whole = jnp.broadcast_to(jnp.sum(total[...], axis=1, keepdims=True), (8, LANES))
    rms_tile = jnp.sqrt(whole / entries + 1e-06)
    share = 1.0 / rms_tile
    for k in range(COMPS):
        for g in range(GROUPS):
            for half in range(2):
                direction[k, 8 * half : 8 * half + 8, lanes(g)] = (
                    back[2 * (k * GROUPS + g) + half] * share
                )
    rms[...] = rms_tile[0:1, :]


def edge_payload(checkpoint, advect, diffuse, rows):
    return jnp.concatenate([checkpoint[:, rows], advect[:, rows], diffuse[None, rows]]).reshape(
        56, COLUMNS
    )


def on_device(checkpoint, advect, diffuse, obs_rows, obs_values, obs_weight, error_inverse, rates):
    initial, flow, spread = checkpoint[0], advect[0], diffuse[0]
    low = passed_along(edge_payload(initial, flow, spread, slice(8, 16)), SPACE, 1)
    high = passed_along(edge_payload(initial, flow, spread, slice(0, 8)), SPACE, -1)
    inverse_rows = jnp.broadcast_to(
        jnp.concatenate([error_inverse[0], error_inverse[0]])[:, None], (8, COLUMNS)
    )
    following = passed_along(
        jnp.concatenate([initial.reshape(64, COLUMNS), inverse_rows]), TM, -1
    )
    history, end_state = pl.pallas_call(
        forward_kernel,
        out_shape=(shape(STEPS, CELLS, ROWS, LANES), shape(CELLS, ROWS, LANES)),
        in_specs=[VMEM] * 5,
        out_specs=(VMEM, VMEM),
        scratch_shapes=[
            pltpu.VMEM((5, GROUPS, TALL, LANES), jnp.float32),
            pltpu.VMEM((2, CELLS, TALL, LANES), jnp.float32),
        ],
        name="forward",
    )(initial, flow, spread, low, high)
    prior_end = passed_along(end_state, TM, 1)
    own, to_low, to_high = pl.pallas_call(
        adjoint_kernel,
        out_shape=(shape(CELLS, ROWS, LANES), shape(CELLS, 8, LANES), shape(CELLS, 8, LANES)),
        in_specs=[SMEM, SMEM] + [VMEM] * 6 + [ANY],
        out_specs=(VMEM, VMEM, VMEM),
        scratch_shapes=[
            pltpu.VMEM((5, GROUPS, TALL, LANES), jnp.float32),
            pltpu.VMEM((2, CELLS, TALL, LANES), jnp.float32),
            pltpu.VMEM((STEPS, 2, COMPS, BLOCK, COLUMNS), jnp.float32),
            pltpu.SemaphoreType.DMA((STEPS,)),
        ],
        name="adjoint",
    )(obs_rows[0], obs_weight, flow, spread, low, high, history, following, obs_values[0])
    from_low = passed_along(to_high, SPACE, 1)
    from_high = passed_along(to_low, SPACE, -1)
    windows = lax.axis_size(TM)
    parcels = pl.pallas_call(
        gradient_kernel,
        out_shape=shape(9 * 2 * CELLS, LANES),
        in_specs=[SMEM] + [VMEM] * 5,
        out_specs=VMEM,
        name="gradient",
    )(error_inverse, own, from_low, from_high, initial, prior_end)
    arrived = lax.all_to_all(
        parcels.reshape(windows, 1, 9 * LANES), TM, split_axis=0, concat_axis=0, tiled=True
    )
    position = lax.axis_index(TM)
    component = (position // (windows // COMPS)).astype(jnp.int32).reshape(1)
    back, total = pl.pallas_call(
        smoothing_kernel,
        out_shape=(shape(windows, 8, LANES), shape(1, LANES)),
        in_specs=[SMEM, SMEM, VMEM],
        out_specs=(VMEM, VMEM),
        name="smoothing",
    )(component, rates, arrived.reshape(9 * windows, LANES))
    back = lax.all_to_all(back, TM, split_axis=0, concat_axis=0, tiled=True)
    total = total + swapped(total, "space_1")
    total = total + swapped(total, "space_0")
    entries = float(windows * lax.axis_size(SPACE) * initial.size)
    direction, rms = pl.pallas_call(
        lambda *refs: final_kernel(entries, *refs),
        out_shape=(shape(COMPS, ROWS, COLUMNS), shape(1, LANES)),
        in_specs=[VMEM, VMEM],
        out_specs=(VMEM, VMEM),
        name="final",
    )(back, total)
    return (direction[None], rms[0, 0])


def solution(mesh):
    torus = Mesh(
        mesh.devices.reshape(8, 2, 4, 2, 2), ("tm_0", "tm_1", "tm_2", "space_0", "space_1")
    )
    return jax.shard_map(
        on_device,
        mesh=torus,
        in_specs=(
            P(TM, None, SPACE, None),
            P(TM, None, SPACE, None),
            P(TM, SPACE, None),
            P(TM, None, SPACE),
            P(TM, None, SPACE, None, None, None),
            P(TM),
            P(TM, None),
            P(),
        ),
        out_specs=(P(TM, None, SPACE, None), P()),
        check_vma=False,
    )
```

time: 258 us -> 99.6 us (0.39)
  starting transfers between devices: 134 us -> 38.5 us
  blocking collectives: 46.6 us -> 0 us
  Pallas kernels: 0 us -> 20.4 us
  matrix products: 13.4 us -> 0 us
  local copies, waits for them, and re-layouts: 16.3 us -> 7.62 us
  waiting for transfers between devices: 33.5 us -> 27.9 us
  other arithmetic: 7.26 us -> 2.98 us
  between operations: 5.02 us -> 1.47 us
    ppermute x34 -> x2, starting transfers between devices: 106 us -> 2.03 us  [swapped(): return lax.ppermute(value, axis, [(0, 1), (1, 0)])]
    psum x5 -> x0, blocking collectives: 46.6 us -> none  [one_axis_at_a_time(): return functools.reduce(lax.psum, axes, x)]
    ppermute x34 -> x2, waiting for transfers between devices: 24.4 us -> 3.66 us  [swapped(): return lax.ppermute(value, axis, [(0, 1), (1, 0)])]
    pallas_call x0 -> x5, Pallas kernels: none -> 20.4 us  [the longest x1 7.93 us: on_device(): pl.pallas_call(adjoint_kernel, out_shape=(shape(CELLS, ROWS, LANES), shap...]
    dot_general x19 -> x0, matrix products: 13.4 us -> none  [the longest x8 7.44 us: select_rows(): jnp.einsum('kb,cbrx->kcrx', picker, blocks, precision=lax.Precision.HIGHEST)]
    ppermute x3 -> x6, starting transfers between devices: 7.5 us -> 17.4 us  [passed_along(): lax.ppermute(value, axis, [(source, source + steps) for source in range(l...]
    ppermute x3 -> x6, waiting for transfers between devices: 0.01 us -> 9.82 us  [passed_along(): lax.ppermute(value, axis, [(source, source + steps) for source in range(l...]
    slice x131 -> x3, local copies, waits for them, and re-layouts: 12.1 us -> 2.66 us  [the longest x1 0.99 us: edge_payload(): checkpoint[:, rows]]
  transfers between devices with their start and end apart: 39 -> 10, of which waited for: 16 -> 7; matrix products, arithmetic and copies ran while one was open for 12% -> 4% of each run, Pallas kernels for 0% -> 15%
where the time goes in v1:
time: 99.6 us; the launch traced here: 98.8 us
  starting transfers between devices  38.5 us (39%)
  waiting for transfers between devices  27.9 us (28%)
  Pallas kernels  20.4 us (20%)
  local copies, waits for them, and re-layouts  7.62 us (8%)
  other arithmetic  2.98 us (3%)
  between operations  1.47 us (1%)
    ppermute x6, starting transfers between devices, passed_along(): lax.ppermute(value, axis, [(source, source + steps) for source in range(l...  17.4 us
    all_to_all x1, starting transfers between devices, on_device(): lax.all_to_all(parcels.reshape(windows, 1, 9 * LANES), TM, split_axis=0,...  14.5 us
    all_to_all x1, waiting for transfers between devices, on_device(): lax.all_to_all(parcels.reshape(windows, 1, 9 * LANES), TM, split_axis=0,...  10.2 us
    ppermute x6, waiting for transfers between devices, passed_along(): lax.ppermute(value, axis, [(source, source + steps) for source in range(l...  9.82 us
    pallas_call x1, Pallas kernels, on_device(): pl.pallas_call(adjoint_kernel, out_shape=(shape(CELLS, ROWS, LANES), shap...  7.93 us
    pallas_call x1, Pallas kernels, on_device(): pl.pallas_call(forward_kernel, out_shape=(shape(STEPS, CELLS, ROWS, LANES...  6.45 us
    all_to_all x1, starting transfers between devices, on_device(): back = lax.all_to_all(back, TM, split_axis=0, concat_axis=0, tiled=True)  4.62 us
    unnamed x21, local copies, waits for them, and re-layouts  4.29 us
  transfers between devices with their start and end apart: 10, of which 7 were waited for; matrix products, arithmetic and copies ran while one was open for 4% of the time, Pallas kernels for 15%

profile of v1, /device:TPU:1, one launch (start us, length us, event | category | flops | bytes accessed | tf_op | source)
XLA Modules:
  0.0 98.8 jit_solution(7015873694822264517)
XLA Ops:
  0.6 1.0 %fusion = (f32[4,8,1024]{2,1,0:T(8,128)S(1)}, f32[4,8,1024]{2,1,0:T(8,128)S(1)}) fusion(f32[4,16,1024]{2,1,0:T(8,128)} %bitcast.17), kind=kLoop, calls=%fused_computation.4 | loop fusion | bytes 524288 | tf_op jit(solution)/shard_map/slice | solution.py:284
  1.6 0.9 fusion.1
  2.5 0.8 fusion.2
  3.3 6.2 %collective-permute-start = (f32[56,1024]{1,0:T(8,128)S(1)}, f32[56,1024]{1,0:T(8,128)S(1)}, u32[]{:S(2)}, u32[]{:S(2)}) collective-permute-start(f32[56,1024]{1,0:T(8,128)S(1)} %maximum_bitcast_fusion), channel_id=1, source_target_pairs={{0,1},{1,2},{2,3},{4,5},{5,6},{6,7},{8,9},{9,10},{10,11},{12,13},{... | collective-permute-start | bytes 688136 | tf_op jit(solution)/shard_map/ppermute | solution.py:38
  9.6 1.9 %collective-permute-start.1 = (f32[56,1024]{1,0:T(8,128)S(1)}, f32[56,1024]{1,0:T(8,128)S(1)}, u32[]{:S(2)}, u32[]{:S(2)}) collective-permute-start(f32[56,1024]{1,0:T(8,128)S(1)} %maximum_bitcast_fusion.1), channel_id=1, source_target_pairs={{1,0},{2,1},{3,2},{5,4},{6,5},{7,6},{9,8},{10,9},{11,10},{13,12},{... | collective-permute-start | bytes 688136 | tf_op jit(solution)/shard_map/ppermute | solution.py:38
  11.5 0.8 pad_maximum_fusion.1
  12.3 1.0 %pad_maximum_fusion = f32[72,1024]{1,0:T(8,128)S(1)} fusion(f32[64,1024]{1,0:T(8,128)} %bitcast.18, f32[72]{0:T(128)S(1)} %pad_maximum_fusion.1), kind=kLoop, calls=%fused_computation | loop fusion | flops 73728 | bytes 557344 | tf_op jit(solution)/shard_map/concatenate | solution.py:297
  13.3 1.3 %collective-permute-start.2 = (f32[72,1024]{1,0:T(8,128)S(1)}, f32[72,1024]{1,0:T(8,128)S(1)}, u32[]{:S(2)}, u32[]{:S(2)}) collective-permute-start(f32[72,1024]{1,0:T(8,128)S(1)} %pad_maximum_fusion), channel_id=1, source_target_pairs={{4,0},{8,4},{12,8},{16,12},{20,16},{24,20},{28,24},{32,28},{36,32}... | collective-permute-start | bytes 884744 | tf_op jit(solution)/shard_map/ppermute | solution.py:38
  14.7 3.7 %collective-permute-done.1.high = f32[56,1024]{1,0:T(8,128)S(1)} collective-permute-done((f32[56,1024]{1,0:T(8,128)S(1)}, f32[56,1024]{1,0:T(8,128)S(1)}, u32[]{:S(2)}, u32[]{:S(2)}) %collective-permute-start.1) | collective-permute-done | bytes 229408 | tf_op jit(solution)/shard_map/ppermute | solution.py:38
  18.4 0.7 copy-done.3
  19.1 6.5 %forward.1 = (f32[8,32,16,128]{3,2,1,0:T(8,128)}, f32[32,16,128]{2,1,0:T(8,128)}) custom-call(f32[4,16,1024]{2,1,0:T(8,128)} %bitcast.19, f32[2,16,1024]{2,1,0:T(8,128)} %bitcast.23, f32[16,1024]{1,0:T(8,128)} %bitcast.27, f32[56,1024]{1,0:T(8,128)} %copy-done.2, f32[56,1024]{1,0:T(8,128)} %copy-done.3), custom_call_target="tpu_custom_call" | custom-call | tf_op jit(solution)/shard_map/forward/pallas_call | solution.py:299
  25.5 3.1 %collective-permute-start.5 = (f32[32,16,128]{2,1,0:T(8,128)}, f32[32,16,128]{2,1,0:T(8,128)S(1)}, u32[]{:S(2)}, u32[]{:S(2)}) collective-permute-start(f32[32,16,128]{2,1,0:T(8,128)} %get-tuple-element.15), channel_id=1, source_target_pairs={{0,4},{4,8},{8,12},{12,16},{16,20},{20,24},{24,28},{28,32},{32,36}... | collective-permute-start | bytes 786440 | tf_op jit(solution)/shard_map/ppermute | solution.py:38
  28.7 0.7 copy.12.obs_rows
  30.0 0.7 copy-done.4
  30.7 7.9 %adjoint.1 = (f32[32,16,128]{2,1,0:T(8,128)}, f32[32,8,128]{2,1,0:T(8,128)}, f32[32,8,128]{2,1,0:T(8,128)}) custom-call(s32[8,2]{1,0:T(8,128)} %copy.12.obs_rows, f32[1]{0:T(128)S(6)} %copy.15.weight, f32[2,16,1024]{2,1,0:T(8,128)} %bitcast.24, f32[16,1024]{1,0:T(8,128)} %bitcast.28, f32[56,1024]{1,0:T(8,128)} %copy-done.2, f32[56,1024]{1,0:T(8,128)} %copy-done.3, ...), custom_call_target="tpu_custom_call" | custom-call | tf_op jit(solution)/shard_map/adjoint/pallas_call | solution.py:311
  38.7 2.9 %collective-permute-start.3 = (f32[32,8,128]{2,1,0:T(8,128)}, f32[32,8,128]{2,1,0:T(8,128)S(1)}, u32[]{:S(2)}, u32[]{:S(2)}) collective-permute-start(f32[32,8,128]{2,1,0:T(8,128)} %get-tuple-element.13), channel_id=1, source_target_pairs={{0,1},{1,2},{2,3},{4,5},{5,6},{6,7},{8,9},{9,10},{10,11},{12,13},{... | collective-permute-start | bytes 393224 | tf_op jit(solution)/shard_map/ppermute | solution.py:38
  41.6 1.9 %collective-permute-start.4 = (f32[32,8,128]{2,1,0:T(8,128)}, f32[32,8,128]{2,1,0:T(8,128)S(1)}, u32[]{:S(2)}, u32[]{:S(2)}) collective-permute-start(f32[32,8,128]{2,1,0:T(8,128)} %get-tuple-element.14), channel_id=1, source_target_pairs={{1,0},{2,1},{3,2},{5,4},{6,5},{7,6},{9,8},{10,9},{11,10},{13,12},{... | collective-permute-start | bytes 393224 | tf_op jit(solution)/shard_map/ppermute | solution.py:38
  43.8 5.8 %collective-permute-done.4.from_high = f32[32,8,128]{2,1,0:T(8,128)S(1)} collective-permute-done((f32[32,8,128]{2,1,0:T(8,128)}, f32[32,8,128]{2,1,0:T(8,128)S(1)}, u32[]{:S(2)}, u32[]{:S(2)}) %collective-permute-start.4) | collective-permute-done | bytes 131104 | tf_op jit(solution)/shard_map/ppermute | solution.py:38
  49.6 0.6 copy-done.7
  50.4 2.0 %gradient.1 = f32[576,128]{1,0:T(8,128)} custom-call(f32[1,4]{1,0:T(1,128)} %inverse.1, f32[32,16,128]{2,1,0:T(8,128)} %get-tuple-element.12.own, f32[32,8,128]{2,1,0:T(8,128)} %copy-done.6, f32[32,8,128]{2,1,0:T(8,128)} %copy-done.7, f32[4,16,1024]{2,1,0:T(8,128)} %bitcast.20, f32[32,16,128]{2,1,0:T(8,128)} %copy-done.5), custom_call_target="tpu_custom_call" | custom-call | tf_op jit(solution)/shard_map/gradient/pallas_call | solution.py:327
  52.4 14.5 %all-to-all-start = ((f32[64,1,1152]{2,1,0:T(1,128)}), f32[64,1,1152]{2,1,0:T(1,128)S(1)}, u32[]{:S(2)}, u32[]{:S(2)}) async-start(f32[64,1,1152]{2,1,0:T(1,128)} %bitcast.25), calls=%async_computation | async-start | bytes 589824 | tf_op jit(solution)/shard_map/all_to_all | solution.py:334
  66.9 0.7 copy.14.rates
  67.6 10.2 %all-to-all-done = f32[64,1,1152]{2,1,0:T(1,128)S(1)} async-done(((f32[64,1,1152]{2,1,0:T(1,128)}), f32[64,1,1152]{2,1,0:T(1,128)S(1)}, u32[]{:S(2)}, u32[]{:S(2)}) %all-to-all-start) | async-done | bytes 294944 | tf_op jit(solution)/shard_map/all_to_all | solution.py:334
  77.8 0.7 copy-done
  78.6 2.2 %smoothing.1 = (f32[64,8,128]{2,1,0:T(8,128)}, f32[1,128]{1,0:T(1,128)}) custom-call(s32[1]{0:T(128)} %bitcast.component, f32[64,4]{1,0:T(8,128)} %copy.14.rates, f32[576,128]{1,0:T(8,128)} %bitcast.26), custom_call_target="tpu_custom_call" | custom-call | tf_op jit(solution)/shard_map/smoothing/pallas_call | solution.py:339
  80.7 4.6 %all-to-all-start.1 = ((f32[64,8,128]{2,1,0:T(8,128)}), f32[64,8,128]{2,1,0:T(8,128)S(1)}, u32[]{:S(2)}, u32[]{:S(2)}) async-start(f32[64,8,128]{2,1,0:T(8,128)} %get-tuple-element.16), calls=%async_computation.1 | async-start | bytes 524288 | tf_op jit(solution)/shard_map/all_to_all | solution.py:346
  85.5 1.4 %collective-permute-done.6 = f32[1,128]{1,0:T(1,128)S(1)} collective-permute-done((f32[1,128]{1,0:T(1,128)}, f32[1,128]{1,0:T(1,128)S(1)}, u32[]{:S(2)}, u32[]{:S(2)}) %collective-permute-start.6) | collective-permute-done | bytes 544 | tf_op jit(solution)/shard_map/ppermute | solution.py:42
  87.4 1.9 %collective-permute-start.7 = (f32[1,128]{1,0:T(1,128)S(1)}, f32[1,128]{1,0:T(1,128)S(1)}, u32[]{:S(2)}, u32[]{:S(2)}) collective-permute-start(f32[1,128]{1,0:T(1,128)S(1)} %add.15), channel_id=1, source_target_pairs={{0,2},{2,0},{1,3},{3,1},{4,6},{6,4},{5,7},{7,5},{8,10},{10,8},{9,1... | collective-permute-start | bytes 1544 | tf_op jit(solution)/shard_map/ppermute | solution.py:42
  89.4 2.3 %collective-permute-done.7 = f32[1,128]{1,0:T(1,128)S(1)} collective-permute-done((f32[1,128]{1,0:T(1,128)S(1)}, f32[1,128]{1,0:T(1,128)S(1)}, u32[]{:S(2)}, u32[]{:S(2)}) %collective-permute-start.7) | collective-permute-done | bytes 544 | tf_op jit(solution)/shard_map/ppermute | solution.py:42
  92.2 4.2 %all-to-all-done.1.refs_0_ = f32[64,8,128]{2,1,0:T(8,128)S(1)} async-done(((f32[64,8,128]{2,1,0:T(8,128)}), f32[64,8,128]{2,1,0:T(8,128)S(1)}, u32[]{:S(2)}, u32[]{:S(2)}) %all-to-all-start.1) | async-done | bytes 262176 | tf_op jit(solution)/shard_map/all_to_all | solution.py:346
  96.4 0.7 copy-done.1
  97.1 1.8 %final.1 = (f32[4,16,1024]{2,1,0:T(8,128)}, f32[1,128]{1,0:T(1,128)}) custom-call(f32[64,8,128]{2,1,0:T(8,128)} %copy-done.1, f32[1,128]{1,0:T(1,128)} %add.16.refs_1_), custom_call_target="tpu_custom_call" | custom-call | tf_op jit(solution)/shard_map/final/pallas_call | solution.py:350
  (24 shorter events, 1.7 us)
Async XLA Ops:
  0.6 28.0 %copy-start.9 = (s32[1,8,2]{1,2,0:T(2,128)S(1)}, s32[1,8,2]{1,2,0:T(2,128)}, u32[]{:S(2)}) copy-start(s32[1,8,2]{1,2,0:T(2,128)} %param.11) | copy-start | bytes 196
  3.3 11.3 %collective-permute-start = (f32[56,1024]{1,0:T(8,128)S(1)}, f32[56,1024]{1,0:T(8,128)S(1)}, u32[]{:S(2)}, u32[]{:S(2)}) collective-permute-start(f32[56,1024]{1,0:T(8,128)S(1)} %maximum_bitcast_fusion), channel_id=1, source_target_pairs={{0,1},{1,2},{2,3},{4,5},{5,6},{6,7},{8,9},{9,10},{10,11},{12,13},{... | collective-permute-start | bytes 688136 | tf_op jit(solution)/shard_map/ppermute | solution.py:38
  9.6 8.8 %collective-permute-start.1 = (f32[56,1024]{1,0:T(8,128)S(1)}, f32[56,1024]{1,0:T(8,128)S(1)}, u32[]{:S(2)}, u32[]{:S(2)}) collective-permute-start(f32[56,1024]{1,0:T(8,128)S(1)} %maximum_bitcast_fusion.1), channel_id=1, source_target_pairs={{1,0},{2,1},{3,2},{5,4},{6,5},{7,6},{9,8},{10,9},{11,10},{13,12},{... | collective-permute-start | bytes 688136 | tf_op jit(solution)/shard_map/ppermute | solution.py:38
  13.3 16.7 %collective-permute-start.2 = (f32[72,1024]{1,0:T(8,128)S(1)}, f32[72,1024]{1,0:T(8,128)S(1)}, u32[]{:S(2)}, u32[]{:S(2)}) collective-permute-start(f32[72,1024]{1,0:T(8,128)S(1)} %pad_maximum_fusion), channel_id=1, source_target_pairs={{4,0},{8,4},{12,8},{16,12},{20,16},{24,20},{28,24},{32,28},{36,32}... | collective-permute-start | bytes 884744 | tf_op jit(solution)/shard_map/ppermute | solution.py:38
  14.6 3.8 %copy-start.2 = (f32[56,1024]{1,0:T(8,128)}, f32[56,1024]{1,0:T(8,128)S(1)}, u32[]{:S(2)}) copy-start(f32[56,1024]{1,0:T(8,128)S(1)} %collective-permute-done.low) | copy-start | bytes 688132
  18.4 0.7 copy-start.3
  25.5 24.1 %collective-permute-start.5 = (f32[32,16,128]{2,1,0:T(8,128)}, f32[32,16,128]{2,1,0:T(8,128)S(1)}, u32[]{:S(2)}, u32[]{:S(2)}) collective-permute-start(f32[32,16,128]{2,1,0:T(8,128)} %get-tuple-element.15), channel_id=1, source_target_pairs={{0,4},{4,8},{8,12},{12,16},{16,20},{20,24},{24,28},{28,32},{32,36}... | collective-permute-start | bytes 786440 | tf_op jit(solution)/shard_map/ppermute | solution.py:38
  30.0 0.7 copy-start.4
  30.7 36.2 %copy-start.8 = (f32[64,4]{0,1:T(4,128)S(1)}, f32[64,4]{0,1:T(4,128)}, u32[]{:S(2)}) copy-start(f32[64,4]{0,1:T(4,128)} %param.15) | copy-start | bytes 3076
  38.7 5.2 %collective-permute-start.3 = (f32[32,8,128]{2,1,0:T(8,128)}, f32[32,8,128]{2,1,0:T(8,128)S(1)}, u32[]{:S(2)}, u32[]{:S(2)}) collective-permute-start(f32[32,8,128]{2,1,0:T(8,128)} %get-tuple-element.13), channel_id=1, source_target_pairs={{0,1},{1,2},{2,3},{4,5},{5,6},{6,7},{8,9},{9,10},{10,11},{12,13},{... | collective-permute-start | bytes 393224 | tf_op jit(solution)/shard_map/ppermute | solution.py:38
  41.6 8.0 %collective-permute-start.4 = (f32[32,8,128]{2,1,0:T(8,128)}, f32[32,8,128]{2,1,0:T(8,128)S(1)}, u32[]{:S(2)}, u32[]{:S(2)}) collective-permute-start(f32[32,8,128]{2,1,0:T(8,128)} %get-tuple-element.14), channel_id=1, source_target_pairs={{1,0},{2,1},{3,2},{5,4},{6,5},{7,6},{9,8},{10,9},{11,10},{13,12},{... | collective-permute-start | bytes 393224 | tf_op jit(solution)/shard_map/ppermute | solution.py:38
  43.8 5.8 %copy-start.6 = (f32[32,8,128]{2,1,0:T(8,128)}, f32[32,8,128]{2,1,0:T(8,128)S(1)}, u32[]{:S(2)}) copy-start(f32[32,8,128]{2,1,0:T(8,128)S(1)} %collective-permute-done.3.from_low) | copy-start | bytes 393220
  49.6 0.6 copy-start.7
  49.6 0.7 copy-start.5
  52.4 25.4 %all-to-all-start = ((f32[64,1,1152]{2,1,0:T(1,128)}), f32[64,1,1152]{2,1,0:T(1,128)S(1)}, u32[]{:S(2)}, u32[]{:S(2)}) async-start(f32[64,1,1152]{2,1,0:T(1,128)} %bitcast.25), calls=%async_computation | async-start | bytes 589824 | tf_op jit(solution)/shard_map/all_to_all | solution.py:334
  77.8 0.7 copy-start
  80.7 15.6 %all-to-all-start.1 = ((f32[64,8,128]{2,1,0:T(8,128)}), f32[64,8,128]{2,1,0:T(8,128)S(1)}, u32[]{:S(2)}, u32[]{:S(2)}) async-start(f32[64,8,128]{2,1,0:T(8,128)} %get-tuple-element.16), calls=%async_computation.1 | async-start | bytes 524288 | tf_op jit(solution)/shard_map/all_to_all | solution.py:346
  85.4 1.5 %collective-permute-start.6 = (f32[1,128]{1,0:T(1,128)}, f32[1,128]{1,0:T(1,128)S(1)}, u32[]{:S(2)}, u32[]{:S(2)}) collective-permute-start(f32[1,128]{1,0:T(1,128)} %get-tuple-element.17), channel_id=1, source_target_pairs={{0,1},{1,0},{2,3},{3,2},{4,5},{5,4},{6,7},{7,6},{8,9},{9,8},{10,11... | collective-permute-start | bytes 1544 | tf_op jit(solution)/shard_map/ppermute | solution.py:42
  87.4 4.2 %collective-permute-start.7 = (f32[1,128]{1,0:T(1,128)S(1)}, f32[1,128]{1,0:T(1,128)S(1)}, u32[]{:S(2)}, u32[]{:S(2)}) collective-permute-start(f32[1,128]{1,0:T(1,128)S(1)} %add.15), channel_id=1, source_target_pairs={{0,2},{2,0},{1,3},{3,1},{4,6},{6,4},{5,7},{7,5},{8,10},{10,8},{9,1... | collective-permute-start | bytes 1544 | tf_op jit(solution)/shard_map/ppermute | solution.py:42
  96.4 0.7 copy-start.1

commit v2 on v1

v2 whole, which is shorter than its diff:
```python
import jax
import jax.numpy as jnp
from jax import lax
from jax.experimental import pallas as pl
from jax.experimental.pallas import tpu as pltpu
from jax.sharding import Mesh
from jax.sharding import PartitionSpec as P

STEPS = 8
BLOCK = 8
COMPS = 4
ROWS = 16
LANES = 128
GROUPS = 8
COLUMNS = GROUPS * LANES
TALL = 48
FIRST = 8
OWN = 16
CELLS = COMPS * GROUPS
SPACE = ("space_0", "space_1")
TM = ("tm_0", "tm_1", "tm_2")
VMEM = pl.BlockSpec(memory_space=pltpu.VMEM)
SMEM = pl.BlockSpec(memory_space=pltpu.SMEM)
FAR = pl.BlockSpec(memory_space=pltpu.HBM)
GRANT = pltpu.CompilerParams(vmem_limit_bytes=8 * 1024 * 1024)


def shape(*dims):
    return jax.ShapeDtypeStruct(dims, jnp.float32)


def local(*dims):
    return pltpu.VMEM(dims, jnp.float32)


def near(value):
    return pltpu.with_memory_space_constraint(value, pltpu.VMEM)


def far(value):
    return pltpu.with_memory_space_constraint(value, pltpu.HBM)


def scalars(value):
    return pltpu.with_memory_space_constraint(value, pltpu.SMEM)


def lanes(group):
    return slice(group * LANES, (group + 1) * LANES)


def passed_along(value, axis, steps):
    count = lax.axis_size(axis)
    leading, last = (max(0, -steps), min(count, count - steps))
    return lax.ppermute(value, axis, [(source, source + steps) for source in range(leading, last)])


def swapped(value, axis):
    return lax.ppermute(value, axis, [(0, 1), (1, 0)])


def crossed(value):
    return lax.ppermute(value, SPACE, [(1, 2), (2, 1)])


def side_rows():
    odd = lax.axis_index("space_1")
    return pl.multiple_of(32 - 24 * odd, 8), pl.multiple_of(8 + 24 * odd, 8)


def eastern(tiles, lane):
    turned = [pltpu.roll(tile, LANES - 1, 1) for tile in tiles]
    return [
        jnp.where(lane == LANES - 1, turned[(g + 1) % GROUPS], turned[g]) for g in range(GROUPS)
    ]


def western(tiles, lane):
    turned = [pltpu.roll(tile, 1, 1) for tile in tiles]
    return [jnp.where(lane == 0, turned[g - 1], turned[g]) for g in range(GROUPS)]


def coefficient_tiles(advect, diffuse, pair, other, tile, group):
    if tile < 2:
        rows = slice(tile * 8, tile * 8 + 8)
        east_flow = advect[0, rows, lanes(group)]
        north_flow = advect[1, rows, lanes(group)]
        spread = diffuse[rows, lanes(group)]
    else:
        side = pair if tile == 2 else other
        east_flow = side[32:40, lanes(group)]
        north_flow = side[40:48, lanes(group)]
        spread = side[48:56, lanes(group)]
    return (
        1.0 - 4.0 * spread,
        spread - 0.5 * east_flow,
        spread + 0.5 * east_flow,
        spread - 0.5 * north_flow,
        spread + 0.5 * north_flow,
    )


def lane_index():
    return lax.broadcasted_iota(jnp.int32, (8, LANES), 1)


def stencil_tile(source, lane, centre, east, west, north, south, store):
    fields = [[source(k, g, 0) for g in range(GROUPS)] for k in range(COMPS)]
    to_east = [eastern(row, lane) for row in fields]
    to_west = [western(row, lane) for row in fields]
    for g in range(GROUPS):
        c, e, w, n, s = centre(g), east(g), west(g), north(g), south(g)
        for k in range(COMPS):
            store(
                k,
                g,
                c * fields[k][g]
                + e * to_east[k][g]
                + w * to_west[k][g]
                + n * source(k, g, 1)
                + s * source(k, g, -1),
            )


def edges_kernel(
    inverse, checkpoint, advect, diffuse,
    to_pair, to_other, to_prior, own_checkpoint, own_advect, own_diffuse, settings,
    inverse_row, arrivals,
):
    copies = []

    def fetch(source, target):
        copies.append(pltpu.make_async_copy(source, target, arrivals.at[len(copies)]))
        copies[-1].start()

    fetch(inverse, inverse_row)
    odd = lax.axis_index("space_1")
    for half, side in ((odd, to_other), (1 - odd, to_pair)):
        rows = pl.ds(pl.multiple_of(8 * half, 8), 8)
        for k in range(COMPS):
            fetch(checkpoint.at[k, rows], side.at[pl.ds(8 * k, 8)])
        for axis in range(2):
            fetch(advect.at[axis, rows], side.at[pl.ds(32 + 8 * axis, 8)])
        fetch(diffuse.at[rows], side.at[pl.ds(48, 8)])
    fetch(checkpoint, to_prior.at[pl.ds(0, COMPS)])
    fetch(checkpoint, own_checkpoint)
    fetch(advect, own_advect)
    fetch(diffuse, own_diffuse)
    copies[0].wait()
    for k in range(COMPS):
        spread = jnp.broadcast_to(inverse_row[0:1, k : k + 1], (8, LANES))
        to_prior[COMPS, 0:8, lanes(k)] = spread
        settings[k] = spread
    for copy in copies[1:]:
        copy.wait()


def forward_kernel(
    checkpoint, advect, diffuse, pair, other, obs_values,
    history, last, observed, coefs, work, arrival,
):
    fetch = pltpu.make_async_copy(obs_values, observed, arrival)
    fetch.start()
    lane = lane_index()
    nothing = jnp.zeros((8, LANES), jnp.float32)
    starts = (OWN, OWN + 8) + side_rows()
    for g in range(GROUPS):
        for tile in range(4):
            rows = pl.ds(starts[tile], 8)
            values = coefficient_tiles(advect, diffuse, pair, other, tile, g)
            for which in range(5):
                coefs[which, g, rows, :] = values[which]
            for k in range(COMPS):
                if tile < 2:
                    value = checkpoint[k, tile * 8 : tile * 8 + 8, lanes(g)]
                else:
                    value = (pair if tile == 2 else other)[8 * k : 8 * k + 8, lanes(g)]
                work[0, k * GROUPS + g, rows, :] = value
        for k in range(COMPS):
            for slot in range(2):
                work[slot, k * GROUPS + g, 0:8, :] = nothing
                work[slot, k * GROUPS + g, TALL - 8 : TALL, :] = nothing

    def step(moment, carry):
        now = lax.rem(moment, 2)
        after = 1 - now
        for tile in range(4):
            start = FIRST + 8 * tile

            def source(k, g, shift):
                return work[now, k * GROUPS + g, start + shift : start + shift + 8, :]

            def store(k, g, value):
                work[after, k * GROUPS + g, start : start + 8, :] = value
                if tile in (1, 2):
                    history[moment, k * GROUPS + g, (tile - 1) * 8 : tile * 8, :] = value

            loads = [
                lambda g, which=which: coefs[which, g, start : start + 8, :] for which in range(5)
            ]
            stencil_tile(source, lane, *loads, store)
        return carry

    lax.fori_loop(0, STEPS, step, 0)
    for cell in range(CELLS):
        last[cell] = history[STEPS - 1, cell]
    fetch.wait()


def adjoint_kernel(
    obs_rows, weight, advect, diffuse, pair, other, history, following, obs_values,
    own, to_pair, to_other, coefs, work,
):
    lane = lane_index()
    nothing = jnp.zeros((8, LANES), jnp.float32)
    starts = (OWN, OWN + 8) + side_rows()
    for tile in range(4):
        rows = pl.ds(starts[tile], 8)
        groups = [
            coefficient_tiles(advect, diffuse, pair, other, tile, g) for g in range(GROUPS)
        ]
        from_east = eastern([values[2] for values in groups], lane)
        from_west = western([values[1] for values in groups], lane)
        for g in range(GROUPS):
            coefs[0, g, rows, :] = groups[g][0]
            coefs[1, g, rows, :] = from_east[g]
            coefs[2, g, rows, :] = from_west[g]
            coefs[3, g, rows, :] = groups[g][4]
            coefs[4, g, rows, :] = groups[g][3]
    inverses = [following[COMPS, 0:8, lanes(k)] for k in range(COMPS)]
    for g in range(GROUPS):
        for which in (3, 4):
            coefs[which, g, 0:8, :] = nothing
            coefs[which, g, TALL - 8 : TALL, :] = nothing
        for k in range(COMPS):
            cell = k * GROUPS + g
            for slot in range(2):
                work[slot, cell, 0:8, :] = nothing
                work[slot, cell, TALL - 8 : TALL, :] = nothing
            work[0, cell, 8:16, :] = nothing
            work[0, cell, 32:40, :] = nothing
            for half in range(2):
                start = following[k, 8 * half : 8 * half + 8, lanes(g)]
                end = history[STEPS - 1, cell, 8 * half : 8 * half + 8, :]
                work[0, cell, OWN + 8 * half : OWN + 8 * half + 8, :] = inverses[k] * (end - start)
    scale = jnp.broadcast_to(weight[...], (8, LANES))

    def step(turn, carry):
        moment = STEPS - 1 - turn
        now = lax.rem(turn, 2)
        after = 1 - now
        for entry in range(2):
            offset = pl.multiple_of(obs_rows[entry, moment] * BLOCK, BLOCK)
            for k in range(COMPS):
                for g in range(GROUPS):
                    cell = k * GROUPS + g
                    misfit = (
                        history[moment, cell, pl.ds(offset, 8), :]
                        - obs_values[moment, entry, k, :, lanes(g)]
                    )
                    there = pl.ds(OWN + offset, 8)
                    work[now, cell, there, :] = work[now, cell, there, :] + scale * misfit
        for tile in range(4):
            start = FIRST + 8 * tile

            def source(k, g, shift):
                return work[now, k * GROUPS + g, start + shift : start + shift + 8, :]

            def store(k, g, value):
                work[after, k * GROUPS + g, start : start + 8, :] = value

            shifts = (0, 0, 0, 1, -1)
            loads = [
                lambda g, which=which: coefs[
                    which, g, start + shifts[which] : start + shifts[which] + 8, :
                ]
                for which in range(5)
            ]
            stencil_tile(source, lane, *loads, store)
        return carry

    lax.fori_loop(0, STEPS, step, 0)
    for cell in range(CELLS):
        to_pair[cell] = work[0, cell, pl.ds(starts[2], 8), :]
        to_other[cell] = work[0, cell, pl.ds(starts[3], 8), :]
        own[cell] = work[0, cell, 16:32, :]


def gradient_kernel(settings, own, from_pair, from_other, checkpoint, prior_end, parcels):
    even = jnp.full((8, LANES), lax.axis_index("space_1")) == 0
    squares = jnp.zeros((8, LANES), jnp.float32)
    for k in range(COMPS):
        scale = settings[k]
        for g in range(GROUPS):
            cell = k * GROUPS + g
            pair, other = from_pair[cell], from_other[cell]
            added = (jnp.where(even, other, pair), jnp.where(even, pair, other))
            for half in range(2):
                rows = slice(8 * half, 8 * half + 8)
                forcing = checkpoint[k, rows, lanes(g)] - prior_end[cell, rows, :]
                value = own[cell, rows, :] + added[half] + scale * forcing
                place = 9 * (2 * cell + half)
                parcels[place : place + 8, :] = value
                squares = squares + value * value
    total = jnp.sum(squares, axis=0, keepdims=True)
    for parcel in range(2 * CELLS):
        parcels[9 * parcel + 8 : 9 * parcel + 9, :] = total


def smoothing_kernel(rates, parcels, back, total):
    windows = back.shape[0]
    which = lax.axis_index(TM) // (windows // COMPS)
    running = jnp.zeros((8, LANES), jnp.float32)
    sums = jnp.zeros((1, LANES), jnp.float32)
    for j in range(windows):
        rate = jnp.full((8, LANES), rates[which, j], jnp.float32)
        innovation = jnp.sqrt(1.0 - rate * rate)
        running = rate * running + innovation * parcels[9 * j : 9 * j + 8, :]
        back[j] = innovation * running
        sums = sums + parcels[9 * j + 8 : 9 * j + 9, :]
    total[...] = sums
    running = back[windows - 1]
    for j in range(windows - 2, -1, -1):
        rate = jnp.full((8, LANES), rates[which, j + 1], jnp.float32)
        running = back[j] + rate * running
        back[j] = running


def final_kernel(entries, back, total, direction, rms):
    whole = jnp.broadcast_to(jnp.sum(total[...], axis=1, keepdims=True), (8, LANES))
    rms_tile = jnp.sqrt(whole / entries + 1e-06)
    share = 1.0 / rms_tile
    for k in range(COMPS):
        for g in range(GROUPS):
            for half in range(2):
                direction[k, 8 * half : 8 * half + 8, lanes(g)] = (
                    back[2 * (k * GROUPS + g) + half] * share
                )
    rms[...] = rms_tile[0:1, :]


def on_device(checkpoint, advect, diffuse, obs_rows, obs_values, obs_weight, error_inverse, rates):
    edge_pair, edge_other, start, initial, flow, spread, settings = pl.pallas_call(
        edges_kernel,
        out_shape=(
            local(56, COLUMNS), local(56, COLUMNS), local(COMPS + 1, ROWS, COLUMNS),
            local(COMPS, ROWS, COLUMNS), local(2, ROWS, COLUMNS), local(ROWS, COLUMNS),
            local(COMPS, 8, LANES),
        ),
        in_specs=[FAR] * 4,
        out_specs=(VMEM,) * 7,
        scratch_shapes=[
            pltpu.VMEM((1, COMPS), jnp.float32),
            pltpu.SemaphoreType.DMA((19,)),
        ],
        name="edges",
        compiler_params=GRANT,
    )(
        far(error_inverse), far(checkpoint[0]), far(advect[0]), far(diffuse[0])
    )
    initial, flow, spread, settings = near(initial), near(flow), near(spread), near(settings)
    other = near(crossed(edge_other))
    pair = near(swapped(edge_pair, "space_1"))
    following = near(passed_along(start, TM, -1))
    weight = near(jnp.broadcast_to(obs_weight[None], (1, LANES)))
    history, end_state, observed = pl.pallas_call(
        forward_kernel,
        out_shape=(
            local(STEPS, CELLS, ROWS, LANES), local(CELLS, ROWS, LANES),
            local(STEPS, 2, COMPS, BLOCK, COLUMNS),
        ),
        in_specs=[VMEM] * 5 + [FAR],
        out_specs=(VMEM,) * 3,
        scratch_shapes=[
            pltpu.VMEM((5, GROUPS, TALL, LANES), jnp.float32),
            pltpu.VMEM((2, CELLS, TALL, LANES), jnp.float32),
            pltpu.SemaphoreType.DMA(()),
        ],
        name="forward",
        compiler_params=GRANT,
    )(initial, flow, spread, pair, other, far(obs_values[0]))
    prior_end = near(passed_along(end_state, TM, 1))
    own, to_pair, to_other = pl.pallas_call(
        adjoint_kernel,
        out_shape=(local(CELLS, ROWS, LANES), local(CELLS, 8, LANES), local(CELLS, 8, LANES)),
        in_specs=[SMEM] + [VMEM] * 8,
        out_specs=(VMEM, VMEM, VMEM),
        scratch_shapes=[
            pltpu.VMEM((5, GROUPS, TALL, LANES), jnp.float32),
            pltpu.VMEM((2, CELLS, TALL, LANES), jnp.float32),
        ],
        name="adjoint",
        compiler_params=GRANT,
    )(
        scalars(obs_rows[0].T), weight, flow, spread, pair, other,
        near(history), following, near(observed),
    )
    from_other = near(crossed(to_other))
    from_pair = near(swapped(to_pair, "space_1"))
    windows = lax.axis_size(TM)
    parcels = pl.pallas_call(
        gradient_kernel,
        out_shape=local(9 * 2 * CELLS, LANES),
        in_specs=[VMEM] * 6,
        out_specs=VMEM,
        name="gradient",
        compiler_params=GRANT,
    )(settings, near(own), from_pair, from_other, initial, prior_end)
    arrived = lax.all_to_all(
        parcels.reshape(windows, 1, 9 * LANES), TM, split_axis=0, concat_axis=0, tiled=True
    )
    back, total = pl.pallas_call(
        smoothing_kernel,
        out_shape=(local(windows, 8, LANES), local(1, LANES)),
        in_specs=[SMEM, VMEM],
        out_specs=(VMEM, VMEM),
        name="smoothing",
        compiler_params=GRANT,
    )(scalars(rates.T), near(arrived.reshape(9 * windows, LANES)))
    back = near(lax.all_to_all(back, TM, split_axis=0, concat_axis=0, tiled=True))
    total = total + swapped(total, "space_1")
    total = near(total + swapped(total, "space_0"))
    entries = float(windows * lax.axis_size(SPACE) * checkpoint.size)
    direction, rms = pl.pallas_call(
        lambda *refs: final_kernel(entries, *refs),
        out_shape=(shape(COMPS, ROWS, COLUMNS), shape(1, LANES)),
        in_specs=[VMEM, VMEM],
        out_specs=(VMEM, VMEM),
        name="final",
        compiler_params=GRANT,
    )(back, total)
    return (direction[None], rms[0, 0])


def solution(mesh):
    torus = Mesh(
        mesh.devices.reshape(8, 2, 4, 2, 2), ("tm_0", "tm_1", "tm_2", "space_0", "space_1")
    )

    return jax.shard_map(
        on_device,
        mesh=torus,
        in_specs=(
            P(TM, None, SPACE, None),
            P(TM, None, SPACE, None),
            P(TM, SPACE, None),
            P(TM, None, SPACE),
            P(TM, None, SPACE, None, None, None),
            P(TM),
            P(TM, None),
            P(),
        ),
        out_specs=(P(TM, None, SPACE, None), P()),
        check_vma=False,
    )
```

time: 99.6 us -> 82.8 us (0.83)
  blocking collectives: 0 us -> 30.1 us
  starting transfers between devices: 38.5 us -> 23.1 us
  waiting for transfers between devices: 27.9 us -> 13.6 us
  local copies, waits for them, and re-layouts: 7.62 us -> 0.01 us
  Pallas kernels: 20.4 us -> 13 us
  other arithmetic: 2.98 us -> 0.01 us
    all_to_all x0 -> x1, blocking collectives: none -> 30.1 us  [on_device(): lax.all_to_all(parcels.reshape(windows, 1, 9 * LANES), TM, split_axis=0,...]
    ppermute x6 -> x2, starting transfers between devices: 17.4 us -> 2.71 us  [passed_along(): lax.ppermute(value, axis, [(source, source + steps) for source in range(l...]
    all_to_all x2 -> x1, starting transfers between devices: 19.1 us -> 4.62 us  [on_device(): lax.all_to_all(back, TM, split_axis=0, concat_axis=0, tiled=True)]
    all_to_all x2 -> x1, waiting for transfers between devices: 14.4 us -> 3.89 us  [on_device(): lax.all_to_all(back, TM, split_axis=0, concat_axis=0, tiled=True)]
    ppermute x6 -> x2, waiting for transfers between devices: 9.82 us -> 0.01 us  [passed_along(): lax.ppermute(value, axis, [(source, source + steps) for source in range(l...]
    ppermute x0 -> x2, starting transfers between devices: none -> 8.01 us  [crossed(): return lax.ppermute(value, SPACE, [(1, 2), (2, 1)])]
    ppermute x0 -> x2, waiting for transfers between devices: none -> 7.27 us  [crossed(): return lax.ppermute(value, SPACE, [(1, 2), (2, 1)])]
    pallas_call x4 -> x5, Pallas kernels: 18.6 us -> 12.2 us  [the longest x1 5.04 us: on_device(): pl.pallas_call(adjoint_kernel, out_shape=(local(CELLS, ROWS, LANES), loca...]
  transfers between devices with their start and end apart: 10 -> 9, of which waited for: 7 -> 5; matrix products, arithmetic and copies ran while one was open for 4% -> 0% of each run, Pallas kernels for 15% -> 11%
where the time goes in v2:
time: 82.8 us; the launch traced here: 81.1 us
  blocking collectives  30.1 us (36%)
  starting transfers between devices  23.1 us (28%)
  waiting for transfers between devices  13.6 us (16%)
  Pallas kernels  13 us (16%)
  between operations  1.42 us (2%)
    all_to_all x1, blocking collectives, on_device(): lax.all_to_all(parcels.reshape(windows, 1, 9 * LANES), TM, split_axis=0,...  30.1 us
    ppermute x2, starting transfers between devices, crossed(): return lax.ppermute(value, SPACE, [(1, 2), (2, 1)])  8.01 us
    ppermute x4, starting transfers between devices, swapped(): return lax.ppermute(value, axis, [(0, 1), (1, 0)])  7.7 us
    ppermute x2, waiting for transfers between devices, crossed(): return lax.ppermute(value, SPACE, [(1, 2), (2, 1)])  7.27 us
    pallas_call x1, Pallas kernels, on_device(): pl.pallas_call(adjoint_kernel, out_shape=(local(CELLS, ROWS, LANES), loca...  5.04 us
    all_to_all x1, starting transfers between devices, on_device(): lax.all_to_all(back, TM, split_axis=0, concat_axis=0, tiled=True)  4.62 us
    pallas_call x1, Pallas kernels, on_device(): pl.pallas_call(forward_kernel, out_shape=(local(STEPS, CELLS, ROWS, LANES...  3.93 us
    all_to_all x1, waiting for transfers between devices, on_device(): lax.all_to_all(back, TM, split_axis=0, concat_axis=0, tiled=True)  3.89 us
  transfers between devices with their start and end apart: 9, of which 5 were waited for; matrix products, arithmetic and copies ran while one was open for 0% of the time, Pallas kernels for 11%

profile of v2, /device:TPU:1, one launch (start us, length us, event | category | flops | bytes accessed | tf_op | source)
XLA Modules:
  0.0 81.1 jit_solution(1133776862234181994)
XLA Ops:
  0.6 0.0 copy-start.1
  0.6 1.5 %edges.1 = (f32[56,1024]{1,0:T(8,128)S(1)}, f32[56,1024]{1,0:T(8,128)S(1)}, f32[5,16,1024]{2,1,0:T(8,128)S(1)}, f32[4,16,1024]{2,1,0:T(8,128)S(1)}, f32[2,16,102...) custom-call(f32[1,4]{1,0:T(1,128)} %inverse.1, f32[4,16,1024]{2,1,0:T(8,128)} %bitcast.20, ...), custom_call_target="tpu_custom_call" | custom-call | tf_op jit(solution)/shard_map/edges/pallas_call | solution.py:343
  2.2 3.3 %collective-permute-start = (f32[56,1024]{1,0:T(8,128)S(1)}, f32[56,1024]{1,0:T(8,128)S(1)}, u32[]{:S(2)}, u32[]{:S(2)}) collective-permute-start(f32[56,1024]{1,0:T(8,128)S(1)} %get-tuple-element.22), channel_id=1, source_target_pairs={{0,1},{1,0},{2,3},{3,2},{4,5},{5,4},{6,7},{7,6},{8,9},{9,8},{10,11... | collective-permute-start | bytes 688136 | tf_op jit(solution)/shard_map/ppermute | solution.py:59
  5.4 3.0 %collective-permute-start.1 = (f32[56,1024]{1,0:T(8,128)S(1)}, f32[56,1024]{1,0:T(8,128)S(1)}, u32[]{:S(2)}, u32[]{:S(2)}) collective-permute-start(f32[56,1024]{1,0:T(8,128)S(1)} %get-tuple-element.23), channel_id=1, source_target_pairs={{1,2},{2,1},{5,6},{6,5},{9,10},{10,9},{13,14},{14,13},{17,18},{18,... | collective-permute-start | bytes 688136 | tf_op jit(solution)/shard_map/ppermute | solution.py:63
  8.5 1.3 %collective-permute-start.2 = (f32[5,16,1024]{2,1,0:T(8,128)S(1)}, f32[5,16,1024]{2,1,0:T(8,128)S(1)}, u32[]{:S(2)}, u32[]{:S(2)}) collective-permute-start(f32[5,16,1024]{2,1,0:T(8,128)S(1)} %get-tuple-element.26), channel_id=1, source_target_pairs={{4,0},{8,4},{12,8},{16,12},{20,16},{24,20},{28,24},{32,28},{36,32}... | collective-permute-start | bytes 983048 | tf_op jit(solution)/shard_map/ppermute | solution.py:55
  9.8 0.0 collective-permute-done.pair
  9.8 4.5 %collective-permute-done.1.other = f32[56,1024]{1,0:T(8,128)S(1)} collective-permute-done((f32[56,1024]{1,0:T(8,128)S(1)}, f32[56,1024]{1,0:T(8,128)S(1)}, u32[]{:S(2)}, u32[]{:S(2)}) %collective-permute-start.1) | collective-permute-done | bytes 229408 | tf_op jit(solution)/shard_map/ppermute | solution.py:63
  14.3 3.9 %forward.1 = (f32[8,32,16,128]{3,2,1,0:T(8,128)S(1)}, f32[32,16,128]{2,1,0:T(8,128)S(1)}, f32[8,2,4,8,1024]{4,3,2,1,0:T(8,128)S(1)}) custom-call(f32[4,16,1024]{2,1,0:T(8,128)S(1)} %get-tuple-element.24.checkpoint, f32[2,16,1024]{2,1,0:T(8,128)S(1)} %get-tuple-element.20.advect, f32[16,1024]{1,0:T(8,128)S(1)} %get-tuple-element.21.diffuse, ...), custom_call_target="tpu_custom_call" | custom-call | tf_op jit(solution)/shard_map/forward/pallas_call | solution.py:366
  18.2 1.4 %collective-permute-start.5 = (f32[32,16,128]{2,1,0:T(8,128)S(1)}, f32[32,16,128]{2,1,0:T(8,128)S(1)}, u32[]{:S(2)}, u32[]{:S(2)}) collective-permute-start(f32[32,16,128]{2,1,0:T(8,128)S(1)} %get-tuple-element.31), channel_id=1, source_target_pairs={{0,4},{4,8},{8,12},{12,16},{16,20},{20,24},{24,28},{28,32},{32,36}... | collective-permute-start | bytes 786440 | tf_op jit(solution)/shard_map/ppermute | solution.py:55
  20.3 0.0 collective-permute-done.2.following
  20.3 0.0 copy-done.1
  20.3 0.0 copy-start
  20.3 5.0 %adjoint.1 = (f32[32,16,128]{2,1,0:T(8,128)S(1)}, f32[32,8,128]{2,1,0:T(8,128)S(1)}, f32[32,8,128]{2,1,0:T(8,128)S(1)}) custom-call(s32[2,8]{1,0:T(2,128)S(1)} %bitcast.18, f32[1,128]{1,0:T(1,128)S(1)} %broadcast_in_dim.12.weight, f32[2,16,1024]{2,1,0:T(8,128)S(1)} %get-tuple-element.20.advect, f32[16,1024]{1,0:T(8,128)S(1)} %get-tuple-element.21.diffuse, ...), custom_call_target="tpu_custom_call" | custom-call | tf_op jit(solution)/shard_map/adjoint/pallas_call | solution.py:383
  25.4 0.1 collective-permute-start.3
  25.5 5.0 %collective-permute-start.4 = (f32[32,8,128]{2,1,0:T(8,128)S(1)}, f32[32,8,128]{2,1,0:T(8,128)S(1)}, u32[]{:S(2)}, u32[]{:S(2)}) collective-permute-start(f32[32,8,128]{2,1,0:T(8,128)S(1)} %get-tuple-element.30), channel_id=1, source_target_pairs={{1,2},{2,1},{5,6},{6,5},{9,10},{10,9},{13,14},{14,13},{17,18},{18,... | collective-permute-start | bytes 393224 | tf_op jit(solution)/shard_map/ppermute | solution.py:63
  30.5 0.0 collective-permute-done.3.from_pair
  30.5 2.8 %collective-permute-done.4.from_other = f32[32,8,128]{2,1,0:T(8,128)S(1)} collective-permute-done((f32[32,8,128]{2,1,0:T(8,128)S(1)}, f32[32,8,128]{2,1,0:T(8,128)S(1)}, u32[]{:S(2)}, u32[]{:S(2)}) %collective-permute-start.4) | collective-permute-done | bytes 131104 | tf_op jit(solution)/shard_map/ppermute | solution.py:63
  33.3 0.0 collective-permute-done.5.prior_end
  33.3 0.1 gradient.1
  33.4 30.1 %all_to_all.10 = f32[64,1,1152]{2,1,0:T(1,128)S(1)} all-to-all(f32[64,1,1152]{2,1,0:T(1,128)S(1)} %bitcast.16), channel_id=1, replica_groups=mesh['tm_0'=8,'tm_1'=2,'tm_2'=4,'space_0'=2,'space_1'=2] {'tm_0','tm_1',..., dimensions={0} | all-to-all | bytes 589824 | tf_op jit(solution)/shard_map/all_to_all | solution.py:409
  63.5 0.0 copy-done
  63.5 1.6 %smoothing.1 = (f32[64,8,128]{2,1,0:T(8,128)}, f32[1,128]{1,0:T(1,128)S(1)}) custom-call(f32[4,64]{1,0:T(4,128)S(1)} %bitcast.17, f32[576,128]{1,0:T(8,128)S(1)} %bitcast.15), custom_call_target="tpu_custom_call" | custom-call | tf_op jit(solution)/shard_map/smoothing/pallas_call | solution.py:412
  65.0 4.6 %all-to-all-start.1 = ((f32[64,8,128]{2,1,0:T(8,128)}), f32[64,8,128]{2,1,0:T(8,128)S(1)}, u32[]{:S(2)}, u32[]{:S(2)}) async-start(f32[64,8,128]{2,1,0:T(8,128)} %get-tuple-element.32), calls=%async_computation.1 | async-start | bytes 524288 | tf_op jit(solution)/shard_map/all_to_all | solution.py:420
  69.7 0.1 collective-permute-start.6
  69.8 1.1 %collective-permute-done.6 = f32[1,128]{1,0:T(1,128)S(1)} collective-permute-done((f32[1,128]{1,0:T(1,128)S(1)}, f32[1,128]{1,0:T(1,128)S(1)}, u32[]{:S(2)}, u32[]{:S(2)}) %collective-permute-start.6) | collective-permute-done | bytes 544 | tf_op jit(solution)/shard_map/ppermute | solution.py:59
  70.9 4.2 %collective-permute-start.7 = (f32[1,128]{1,0:T(1,128)S(1)}, f32[1,128]{1,0:T(1,128)S(1)}, u32[]{:S(2)}, u32[]{:S(2)}) collective-permute-start(f32[1,128]{1,0:T(1,128)S(1)} %add.6), channel_id=1, source_target_pairs={{0,2},{2,0},{1,3},{3,1},{4,6},{6,4},{5,7},{7,5},{8,10},{10,8},{9,1... | collective-permute-start | bytes 1544 | tf_op jit(solution)/shard_map/ppermute | solution.py:59
  75.2 1.3 %collective-permute-done.7 = f32[1,128]{1,0:T(1,128)S(1)} collective-permute-done((f32[1,128]{1,0:T(1,128)S(1)}, f32[1,128]{1,0:T(1,128)S(1)}, u32[]{:S(2)}, u32[]{:S(2)}) %collective-permute-start.7) | collective-permute-done | bytes 544 | tf_op jit(solution)/shard_map/ppermute | solution.py:59
  76.4 3.9 %all-to-all-done.1.refs_0_ = f32[64,8,128]{2,1,0:T(8,128)S(1)} async-done(((f32[64,8,128]{2,1,0:T(8,128)}), f32[64,8,128]{2,1,0:T(8,128)S(1)}, u32[]{:S(2)}, u32[]{:S(2)}) %all-to-all-start.1) | async-done | bytes 262176 | tf_op jit(solution)/shard_map/all_to_all | solution.py:420
  80.3 0.8 %final.1 = (f32[4,16,1024]{2,1,0:T(8,128)}, f32[1,128]{1,0:T(1,128)}) custom-call(f32[64,8,128]{2,1,0:T(8,128)S(1)} %all-to-all-done.1.refs_0_, f32[1,128]{1,0:T(1,128)S(1)} %add.7.refs_1_), custom_call_target="tpu_custom_call" | custom-call | tf_op jit(solution)/shard_map/final/pallas_call | solution.py:424
  (3 shorter events, 0.0 us)
Async XLA Ops:
  0.6 19.7 %copy-start.1 = (s32[1,8,2]{1,2,0:T(2,128)S(1)}, s32[1,8,2]{1,2,0:T(2,128)}, u32[]{:S(2)}) copy-start(s32[1,8,2]{1,2,0:T(2,128)} %param.11) | copy-start | bytes 196
  2.2 7.6 %collective-permute-start = (f32[56,1024]{1,0:T(8,128)S(1)}, f32[56,1024]{1,0:T(8,128)S(1)}, u32[]{:S(2)}, u32[]{:S(2)}) collective-permute-start(f32[56,1024]{1,0:T(8,128)S(1)} %get-tuple-element.22), channel_id=1, source_target_pairs={{0,1},{1,0},{2,3},{3,2},{4,5},{5,4},{6,7},{7,6},{8,9},{9,8},{10,11... | collective-permute-start | bytes 688136 | tf_op jit(solution)/shard_map/ppermute | solution.py:59
  5.4 8.8 %collective-permute-start.1 = (f32[56,1024]{1,0:T(8,128)S(1)}, f32[56,1024]{1,0:T(8,128)S(1)}, u32[]{:S(2)}, u32[]{:S(2)}) collective-permute-start(f32[56,1024]{1,0:T(8,128)S(1)} %get-tuple-element.23), channel_id=1, source_target_pairs={{1,2},{2,1},{5,6},{6,5},{9,10},{10,9},{13,14},{14,13},{17,18},{18,... | collective-permute-start | bytes 688136 | tf_op jit(solution)/shard_map/ppermute | solution.py:63
  8.5 11.8 %collective-permute-start.2 = (f32[5,16,1024]{2,1,0:T(8,128)S(1)}, f32[5,16,1024]{2,1,0:T(8,128)S(1)}, u32[]{:S(2)}, u32[]{:S(2)}) collective-permute-start(f32[5,16,1024]{2,1,0:T(8,128)S(1)} %get-tuple-element.26), channel_id=1, source_target_pairs={{4,0},{8,4},{12,8},{16,12},{20,16},{24,20},{28,24},{32,28},{36,32}... | collective-permute-start | bytes 983048 | tf_op jit(solution)/shard_map/ppermute | solution.py:55
  18.2 15.1 %collective-permute-start.5 = (f32[32,16,128]{2,1,0:T(8,128)S(1)}, f32[32,16,128]{2,1,0:T(8,128)S(1)}, u32[]{:S(2)}, u32[]{:S(2)}) collective-permute-start(f32[32,16,128]{2,1,0:T(8,128)S(1)} %get-tuple-element.31), channel_id=1, source_target_pairs={{0,4},{4,8},{8,12},{12,16},{16,20},{20,24},{24,28},{28,32},{32,36}... | collective-permute-start | bytes 786440 | tf_op jit(solution)/shard_map/ppermute | solution.py:55
  20.3 43.1 %copy-start = (f32[64,4]{0,1:T(4,128)S(1)}, f32[64,4]{0,1:T(4,128)}, u32[]{:S(2)}) copy-start(f32[64,4]{0,1:T(4,128)} %param.15) | copy-start | bytes 3076
  25.4 5.1 %collective-permute-start.3 = (f32[32,8,128]{2,1,0:T(8,128)S(1)}, f32[32,8,128]{2,1,0:T(8,128)S(1)}, u32[]{:S(2)}, u32[]{:S(2)}) collective-permute-start(f32[32,8,128]{2,1,0:T(8,128)S(1)} %get-tuple-element.29), channel_id=1, source_target_pairs={{0,1},{1,0},{2,3},{3,2},{4,5},{5,4},{6,7},{7,6},{8,9},{9,8},{10,11... | collective-permute-start | bytes 393224 | tf_op jit(solution)/shard_map/ppermute | solution.py:59
  25.5 7.8 %collective-permute-start.4 = (f32[32,8,128]{2,1,0:T(8,128)S(1)}, f32[32,8,128]{2,1,0:T(8,128)S(1)}, u32[]{:S(2)}, u32[]{:S(2)}) collective-permute-start(f32[32,8,128]{2,1,0:T(8,128)S(1)} %get-tuple-element.30), channel_id=1, source_target_pairs={{1,2},{2,1},{5,6},{6,5},{9,10},{10,9},{13,14},{14,13},{17,18},{18,... | collective-permute-start | bytes 393224 | tf_op jit(solution)/shard_map/ppermute | solution.py:63
  65.0 15.3 %all-to-all-start.1 = ((f32[64,8,128]{2,1,0:T(8,128)}), f32[64,8,128]{2,1,0:T(8,128)S(1)}, u32[]{:S(2)}, u32[]{:S(2)}) async-start(f32[64,8,128]{2,1,0:T(8,128)} %get-tuple-element.32), calls=%async_computation.1 | async-start | bytes 524288 | tf_op jit(solution)/shard_map/all_to_all | solution.py:420
  69.7 1.2 %collective-permute-start.6 = (f32[1,128]{1,0:T(1,128)S(1)}, f32[1,128]{1,0:T(1,128)S(1)}, u32[]{:S(2)}, u32[]{:S(2)}) collective-permute-start(f32[1,128]{1,0:T(1,128)S(1)} %get-tuple-element.33), channel_id=1, source_target_pairs={{0,1},{1,0},{2,3},{3,2},{4,5},{5,4},{6,7},{7,6},{8,9},{9,8},{10,11... | collective-permute-start | bytes 1544 | tf_op jit(solution)/shard_map/ppermute | solution.py:59
  70.9 5.5 %collective-permute-start.7 = (f32[1,128]{1,0:T(1,128)S(1)}, f32[1,128]{1,0:T(1,128)S(1)}, u32[]{:S(2)}, u32[]{:S(2)}) collective-permute-start(f32[1,128]{1,0:T(1,128)S(1)} %add.6), channel_id=1, source_target_pairs={{0,2},{2,0},{1,3},{3,1},{4,6},{6,4},{5,7},{7,5},{8,10},{10,8},{9,1... | collective-permute-start | bytes 1544 | tf_op jit(solution)/shard_map/ppermute | solution.py:59

commit v3 on v2

--- a/solution.py
+++ b/solution.py
@@ -17,6 +17,7 @@
 FIRST = 8
 OWN = 16
 CELLS = COMPS * GROUPS
+TOGETHER = 4
 SPACE = ("space_0", "space_1")
 TM = ("tm_0", "tm_1", "tm_2")
 VMEM = pl.BlockSpec(memory_space=pltpu.VMEM)
@@ -104,22 +105,30 @@
     return lax.broadcasted_iota(jnp.int32, (8, LANES), 1)
 
 
-def stencil_tile(source, lane, centre, east, west, north, south, store):
-    fields = [[source(k, g, 0) for g in range(GROUPS)] for k in range(COMPS)]
-    to_east = [eastern(row, lane) for row in fields]
-    to_west = [western(row, lane) for row in fields]
-    for g in range(GROUPS):
-        c, e, w, n, s = centre(g), east(g), west(g), north(g), south(g)
-        for k in range(COMPS):
-            store(
-                k,
-                g,
-                c * fields[k][g]
-                + e * to_east[k][g]
-                + w * to_west[k][g]
-                + n * source(k, g, 1)
-                + s * source(k, g, -1),
-            )
+def stencil_step(source, target, coefs, shifts, first, tiles, lane):
+    def components(turn, carry):
+        for k in range(TOGETHER):
+            cell = (turn * TOGETHER + k) * GROUPS
+            for tile in range(tiles):
+                start = FIRST + first + 8 * tile
+                field = [source[cell + g, start : start + 8, :] for g in range(GROUPS)]
+                to_east = eastern(field, lane)
+                to_west = western(field, lane)
+                for g in range(GROUPS):
+                    c, e, w, n, s = (
+                        coefs[which, g, start + shifts[which] : start + shifts[which] + 8, :]
+                        for which in range(5)
+                    )
+                    target[cell + g, start : start + 8, :] = (
+                        c * field[g]
+                        + e * to_east[g]
+                        + w * to_west[g]
+                        + n * source[cell + g, start + 1 : start + 9, :]
+                        + s * source[cell + g, start - 1 : start + 7, :]
+                    )
+        return carry
+
+    lax.fori_loop(0, COMPS // TOGETHER, components, 0)
 
 
 def edges_kernel(
@@ -157,7 +166,7 @@
 
 def forward_kernel(
     checkpoint, advect, diffuse, pair, other, obs_values,
-    history, last, observed, coefs, work, arrival,
+    history, last, observed, coefs, initial, arrival,
 ):
     fetch = pltpu.make_async_copy(obs_values, observed, arrival)
     fetch.start()
@@ -175,35 +184,19 @@
                     value = checkpoint[k, tile * 8 : tile * 8 + 8, lanes(g)]
                 else:
                     value = (pair if tile == 2 else other)[8 * k : 8 * k + 8, lanes(g)]
-                work[0, k * GROUPS + g, rows, :] = value
+                initial[k * GROUPS + g, rows, :] = value
         for k in range(COMPS):
-            for slot in range(2):
-                work[slot, k * GROUPS + g, 0:8, :] = nothing
-                work[slot, k * GROUPS + g, TALL - 8 : TALL, :] = nothing
-
-    def step(moment, carry):
-        now = lax.rem(moment, 2)
-        after = 1 - now
-        for tile in range(4):
-            start = FIRST + 8 * tile
-
-            def source(k, g, shift):
-                return work[now, k * GROUPS + g, start + shift : start + shift + 8, :]
-
-            def store(k, g, value):
-                work[after, k * GROUPS + g, start : start + 8, :] = value
-                if tile in (1, 2):
-                    history[moment, k * GROUPS + g, (tile - 1) * 8 : tile * 8, :] = value
-
-            loads = [
-                lambda g, which=which: coefs[which, g, start : start + 8, :] for which in range(5)
-            ]
-            stencil_tile(source, lane, *loads, store)
-        return carry
-
-    lax.fori_loop(0, STEPS, step, 0)
+            initial[k * GROUPS + g, 0:8, :] = nothing
+            initial[k * GROUPS + g, TALL - 8 : TALL, :] = nothing
+
+    for moment in range(STEPS):
+        first, tiles = ((0, 4), (4, 3), (8, 2))[(moment >= 3) + (moment >= 7)]
+        if tiles == 3:
+            first = moment + 1
+        source = history.at[moment - 1] if moment else initial
+        stencil_step(source, history.at[moment], coefs, (0,) * 5, first, tiles, lane)
     for cell in range(CELLS):
-        last[cell] = history[STEPS - 1, cell]
+        last[cell] = history[STEPS - 1, cell, OWN : OWN + 16, :]
     fetch.wait()
 
 
@@ -235,51 +228,31 @@
         for k in range(COMPS):
             cell = k * GROUPS + g
             for slot in range(2):
-                work[slot, cell, 0:8, :] = nothing
-                work[slot, cell, TALL - 8 : TALL, :] = nothing
-            work[0, cell, 8:16, :] = nothing
-            work[0, cell, 32:40, :] = nothing
+                for rows in (slice(0, 8), slice(8, 16), slice(32, 40), slice(TALL - 8, TALL)):
+                    work[slot, cell, rows, :] = nothing
             for half in range(2):
                 start = following[k, 8 * half : 8 * half + 8, lanes(g)]
-                end = history[STEPS - 1, cell, 8 * half : 8 * half + 8, :]
+                end = history[STEPS - 1, cell, OWN + 8 * half : OWN + 8 * half + 8, :]
                 work[0, cell, OWN + 8 * half : OWN + 8 * half + 8, :] = inverses[k] * (end - start)
     scale = jnp.broadcast_to(weight[...], (8, LANES))
 
-    def step(turn, carry):
+    for turn in range(STEPS):
         moment = STEPS - 1 - turn
-        now = lax.rem(turn, 2)
-        after = 1 - now
+        now = turn % 2
         for entry in range(2):
             offset = pl.multiple_of(obs_rows[entry, moment] * BLOCK, BLOCK)
+            there = pl.ds(OWN + offset, 8)
             for k in range(COMPS):
                 for g in range(GROUPS):
                     cell = k * GROUPS + g
-                    misfit = (
-                        history[moment, cell, pl.ds(offset, 8), :]
-                        - obs_values[moment, entry, k, :, lanes(g)]
-                    )
-                    there = pl.ds(OWN + offset, 8)
+                    misfit = history[moment, cell, there, :] - obs_values[
+                        moment, entry, k, :, lanes(g)
+                    ]
                     work[now, cell, there, :] = work[now, cell, there, :] + scale * misfit
-        for tile in range(4):
-            start = FIRST + 8 * tile
-
-            def source(k, g, shift):
-                return work[now, k * GROUPS + g, start + shift : start + shift + 8, :]
-
-            def store(k, g, value):
-                work[after, k * GROUPS + g, start : start + 8, :] = value
-
-            shifts = (0, 0, 0, 1, -1)
-            loads = [
-                lambda g, which=which: coefs[
-                    which, g, start + shifts[which] : start + shifts[which] + 8, :
-                ]
-                for which in range(5)
-            ]
-            stencil_tile(source, lane, *loads, store)
-        return carry
-
-    lax.fori_loop(0, STEPS, step, 0)
+        first, tiles = (7 - turn, 3) if turn < 4 else (0, 4)
+        stencil_step(
+            work.at[now], work.at[1 - now], coefs, (0, 0, 0, 1, -1), first, tiles, lane
+        )
     for cell in range(CELLS):
         to_pair[cell] = work[0, cell, pl.ds(starts[2], 8), :]
         to_other[cell] = work[0, cell, pl.ds(starts[3], 8), :]
@@ -366,14 +339,14 @@
     history, end_state, observed = pl.pallas_call(
         forward_kernel,
         out_shape=(
-            local(STEPS, CELLS, ROWS, LANES), local(CELLS, ROWS, LANES),
+            local(STEPS, CELLS, TALL, LANES), local(CELLS, ROWS, LANES),
             local(STEPS, 2, COMPS, BLOCK, COLUMNS),
         ),
         in_specs=[VMEM] * 5 + [FAR],
         out_specs=(VMEM,) * 3,
         scratch_shapes=[
             pltpu.VMEM((5, GROUPS, TALL, LANES), jnp.float32),
-            pltpu.VMEM((2, CELLS, TALL, LANES), jnp.float32),
+            pltpu.VMEM((CELLS, TALL, LANES), jnp.float32),
             pltpu.SemaphoreType.DMA(()),
         ],
         name="forward",

time: 82.8 us -> 80.1 us (0.967)
  the two profiles are of different devices: /device:TPU:1 before, /device:TPU:16 now
where the time goes in v3:
time: 80.1 us; the launch traced here: 79.8 us
  blocking collectives  31.2 us (39%)
  waiting for transfers between devices  20.9 us (26%)
  starting transfers between devices  15.8 us (20%)
  Pallas kernels  10.3 us (13%)
  between operations  1.43 us (2%)
    all_to_all x1, blocking collectives, on_device(): lax.all_to_all(parcels.reshape(windows, 1, 9 * LANES), TM, split_axis=0,...  31.2 us
    ppermute x2, waiting for transfers between devices, crossed(): return lax.ppermute(value, SPACE, [(1, 2), (2, 1)])  9.23 us
    ppermute x4, waiting for transfers between devices, swapped(): return lax.ppermute(value, axis, [(0, 1), (1, 0)])  6.23 us
    ppermute x2, starting transfers between devices, crossed(): return lax.ppermute(value, SPACE, [(1, 2), (2, 1)])  6.07 us
    all_to_all x1, waiting for transfers between devices, on_device(): lax.all_to_all(back, TM, split_axis=0, concat_axis=0, tiled=True)  5.45 us
    all_to_all x1, starting transfers between devices, on_device(): lax.all_to_all(back, TM, split_axis=0, concat_axis=0, tiled=True)  4.79 us
    ppermute x2, starting transfers between devices, passed_along(): lax.ppermute(value, axis, [(source, source + steps) for source in range(l...  4.7 us
    pallas_call x1, Pallas kernels, on_device(): pl.pallas_call(adjoint_kernel, out_shape=(local(CELLS, ROWS, LANES), loca...  3.68 us
  transfers between devices with their start and end apart: 9, of which 5 were waited for; matrix products, arithmetic and copies ran while one was open for 0% of the time, Pallas kernels for 8%

profile of v3, /device:TPU:16, one launch (start us, length us, event | category | flops | bytes accessed | tf_op | source)
XLA Modules:
  0.0 79.8 jit_solution(5189421984419618827)
XLA Ops:
  0.6 0.0 copy-start.1
  0.6 1.5 %edges.1 = (f32[56,1024]{1,0:T(8,128)S(1)}, f32[56,1024]{1,0:T(8,128)S(1)}, f32[5,16,1024]{2,1,0:T(8,128)S(1)}, f32[4,16,1024]{2,1,0:T(8,128)S(1)}, f32[2,16,102...) custom-call(f32[1,4]{1,0:T(1,128)} %inverse.1, f32[4,16,1024]{2,1,0:T(8,128)} %bitcast.20, ...), custom_call_target="tpu_custom_call" | custom-call | tf_op jit(solution)/shard_map/edges/pallas_call | solution.py:316
  2.2 0.1 collective-permute-start
  2.3 4.0 %collective-permute-start.1 = (f32[56,1024]{1,0:T(8,128)S(1)}, f32[56,1024]{1,0:T(8,128)S(1)}, u32[]{:S(2)}, u32[]{:S(2)}) collective-permute-start(f32[56,1024]{1,0:T(8,128)S(1)} %get-tuple-element.23), channel_id=1, source_target_pairs={{1,2},{2,1},{5,6},{6,5},{9,10},{10,9},{13,14},{14,13},{17,18},{18,... | collective-permute-start | bytes 688136 | tf_op jit(solution)/shard_map/ppermute | solution.py:64
  6.3 1.3 %collective-permute-start.2 = (f32[5,16,1024]{2,1,0:T(8,128)S(1)}, f32[5,16,1024]{2,1,0:T(8,128)S(1)}, u32[]{:S(2)}, u32[]{:S(2)}) collective-permute-start(f32[5,16,1024]{2,1,0:T(8,128)S(1)} %get-tuple-element.26), channel_id=1, source_target_pairs={{4,0},{8,4},{12,8},{16,12},{20,16},{24,20},{28,24},{32,28},{36,32}... | collective-permute-start | bytes 983048 | tf_op jit(solution)/shard_map/ppermute | solution.py:56
  7.6 0.0 collective-permute-done.pair
  7.6 3.5 %collective-permute-done.1.other = f32[56,1024]{1,0:T(8,128)S(1)} collective-permute-done((f32[56,1024]{1,0:T(8,128)S(1)}, f32[56,1024]{1,0:T(8,128)S(1)}, u32[]{:S(2)}, u32[]{:S(2)}) %collective-permute-start.1) | collective-permute-done | bytes 229408 | tf_op jit(solution)/shard_map/ppermute | solution.py:64
  11.1 2.6 %forward.1 = (f32[8,32,48,128]{3,2,1,0:T(8,128)S(1)}, f32[32,16,128]{2,1,0:T(8,128)S(1)}, f32[8,2,4,8,1024]{4,3,2,1,0:T(8,128)S(1)}) custom-call(f32[4,16,1024]{2,1,0:T(8,128)S(1)} %get-tuple-element.24.checkpoint, f32[2,16,1024]{2,1,0:T(8,128)S(1)} %get-tuple-element.20.advect, f32[16,1024]{1,0:T(8,128)S(1)} %get-tuple-element.21.diffuse, ...), custom_call_target="tpu_custom_call" | custom-call | tf_op jit(solution)/shard_map/forward/pallas_call | solution.py:339
  13.7 3.4 %collective-permute-start.5 = (f32[32,16,128]{2,1,0:T(8,128)S(1)}, f32[32,16,128]{2,1,0:T(8,128)S(1)}, u32[]{:S(2)}, u32[]{:S(2)}) collective-permute-start(f32[32,16,128]{2,1,0:T(8,128)S(1)} %get-tuple-element.31), channel_id=1, source_target_pairs={{0,4},{4,8},{8,12},{12,16},{16,20},{20,24},{24,28},{28,32},{32,36}... | collective-permute-start | bytes 786440 | tf_op jit(solution)/shard_map/ppermute | solution.py:56
  17.8 0.0 collective-permute-done.2.following
  17.8 0.0 copy-done.1
  17.8 0.0 copy-start
  17.9 3.7 %adjoint.1 = (f32[32,16,128]{2,1,0:T(8,128)S(1)}, f32[32,8,128]{2,1,0:T(8,128)S(1)}, f32[32,8,128]{2,1,0:T(8,128)S(1)}) custom-call(s32[2,8]{1,0:T(2,128)S(1)} %bitcast.18, f32[1,128]{1,0:T(1,128)S(1)} %broadcast_in_dim.12.weight, f32[2,16,1024]{2,1,0:T(8,128)S(1)} %get-tuple-element.20.advect, f32[16,1024]{1,0:T(8,128)S(1)} %get-tuple-element.21.diffuse, ...), custom_call_target="tpu_custom_call" | custom-call | tf_op jit(solution)/shard_map/adjoint/pallas_call | solution.py:356
  21.5 0.1 collective-permute-start.3
  21.6 2.0 %collective-permute-start.4 = (f32[32,8,128]{2,1,0:T(8,128)S(1)}, f32[32,8,128]{2,1,0:T(8,128)S(1)}, u32[]{:S(2)}, u32[]{:S(2)}) collective-permute-start(f32[32,8,128]{2,1,0:T(8,128)S(1)} %get-tuple-element.30), channel_id=1, source_target_pairs={{1,2},{2,1},{5,6},{6,5},{9,10},{10,9},{13,14},{14,13},{17,18},{18,... | collective-permute-start | bytes 393224 | tf_op jit(solution)/shard_map/ppermute | solution.py:64
  23.7 0.0 collective-permute-done.3.from_pair
  23.7 5.7 %collective-permute-done.4.from_other = f32[32,8,128]{2,1,0:T(8,128)S(1)} collective-permute-done((f32[32,8,128]{2,1,0:T(8,128)S(1)}, f32[32,8,128]{2,1,0:T(8,128)S(1)}, u32[]{:S(2)}, u32[]{:S(2)}) %collective-permute-start.4) | collective-permute-done | bytes 131104 | tf_op jit(solution)/shard_map/ppermute | solution.py:64
  29.4 0.0 collective-permute-done.5.prior_end
  29.4 0.1 gradient.1
  29.6 31.2 %all_to_all.10 = f32[64,1,1152]{2,1,0:T(1,128)S(1)} all-to-all(f32[64,1,1152]{2,1,0:T(1,128)S(1)} %bitcast.16), channel_id=1, replica_groups=mesh['tm_0'=8,'tm_1'=2,'tm_2'=4,'space_0'=2,'space_1'=2] {'tm_0','tm_1',..., dimensions={0} | all-to-all | bytes 589824 | tf_op jit(solution)/shard_map/all_to_all | solution.py:382
  60.8 0.0 copy-done
  60.8 1.6 %smoothing.1 = (f32[64,8,128]{2,1,0:T(8,128)}, f32[1,128]{1,0:T(1,128)S(1)}) custom-call(f32[4,64]{1,0:T(4,128)S(1)} %bitcast.17, f32[576,128]{1,0:T(8,128)S(1)} %bitcast.15), custom_call_target="tpu_custom_call" | custom-call | tf_op jit(solution)/shard_map/smoothing/pallas_call | solution.py:385
  62.4 4.8 %all-to-all-start.1 = ((f32[64,8,128]{2,1,0:T(8,128)}), f32[64,8,128]{2,1,0:T(8,128)S(1)}, u32[]{:S(2)}, u32[]{:S(2)}) async-start(f32[64,8,128]{2,1,0:T(8,128)} %get-tuple-element.32), calls=%async_computation.1 | async-start | bytes 524288 | tf_op jit(solution)/shard_map/all_to_all | solution.py:393
  67.2 0.1 collective-permute-start.6
  67.3 1.1 %collective-permute-done.6 = f32[1,128]{1,0:T(1,128)S(1)} collective-permute-done((f32[1,128]{1,0:T(1,128)S(1)}, f32[1,128]{1,0:T(1,128)S(1)}, u32[]{:S(2)}, u32[]{:S(2)}) %collective-permute-start.6) | collective-permute-done | bytes 544 | tf_op jit(solution)/shard_map/ppermute | solution.py:60
  68.4 0.0 collective-permute-start.7
  68.4 5.1 %collective-permute-done.7 = f32[1,128]{1,0:T(1,128)S(1)} collective-permute-done((f32[1,128]{1,0:T(1,128)S(1)}, f32[1,128]{1,0:T(1,128)S(1)}, u32[]{:S(2)}, u32[]{:S(2)}) %collective-permute-start.7) | collective-permute-done | bytes 544 | tf_op jit(solution)/shard_map/ppermute | solution.py:60
  73.5 5.5 %all-to-all-done.1.refs_0_ = f32[64,8,128]{2,1,0:T(8,128)S(1)} async-done(((f32[64,8,128]{2,1,0:T(8,128)}), f32[64,8,128]{2,1,0:T(8,128)S(1)}, u32[]{:S(2)}, u32[]{:S(2)}) %all-to-all-start.1) | async-done | bytes 262176 | tf_op jit(solution)/shard_map/all_to_all | solution.py:393
  79.0 0.8 %final.1 = (f32[4,16,1024]{2,1,0:T(8,128)}, f32[1,128]{1,0:T(1,128)}) custom-call(f32[64,8,128]{2,1,0:T(8,128)S(1)} %all-to-all-done.1.refs_0_, f32[1,128]{1,0:T(1,128)S(1)} %add.7.refs_1_), custom_call_target="tpu_custom_call" | custom-call | tf_op jit(solution)/shard_map/final/pallas_call | solution.py:397
  (3 shorter events, 0.0 us)
Async XLA Ops:
  0.6 17.2 %copy-start.1 = (s32[1,8,2]{1,2,0:T(2,128)S(1)}, s32[1,8,2]{1,2,0:T(2,128)}, u32[]{:S(2)}) copy-start(s32[1,8,2]{1,2,0:T(2,128)} %param.11) | copy-start | bytes 196
  2.2 5.5 %collective-permute-start = (f32[56,1024]{1,0:T(8,128)S(1)}, f32[56,1024]{1,0:T(8,128)S(1)}, u32[]{:S(2)}, u32[]{:S(2)}) collective-permute-start(f32[56,1024]{1,0:T(8,128)S(1)} %get-tuple-element.22), channel_id=1, source_target_pairs={{0,1},{1,0},{2,3},{3,2},{4,5},{5,4},{6,7},{7,6},{8,9},{9,8},{10,11... | collective-permute-start | bytes 688136 | tf_op jit(solution)/shard_map/ppermute | solution.py:60
  2.3 8.8 %collective-permute-start.1 = (f32[56,1024]{1,0:T(8,128)S(1)}, f32[56,1024]{1,0:T(8,128)S(1)}, u32[]{:S(2)}, u32[]{:S(2)}) collective-permute-start(f32[56,1024]{1,0:T(8,128)S(1)} %get-tuple-element.23), channel_id=1, source_target_pairs={{1,2},{2,1},{5,6},{6,5},{9,10},{10,9},{13,14},{14,13},{17,18},{18,... | collective-permute-start | bytes 688136 | tf_op jit(solution)/shard_map/ppermute | solution.py:64
  6.3 11.5 %collective-permute-start.2 = (f32[5,16,1024]{2,1,0:T(8,128)S(1)}, f32[5,16,1024]{2,1,0:T(8,128)S(1)}, u32[]{:S(2)}, u32[]{:S(2)}) collective-permute-start(f32[5,16,1024]{2,1,0:T(8,128)S(1)} %get-tuple-element.26), channel_id=1, source_target_pairs={{4,0},{8,4},{12,8},{16,12},{20,16},{24,20},{28,24},{32,28},{36,32}... | collective-permute-start | bytes 983048 | tf_op jit(solution)/shard_map/ppermute | solution.py:56
  13.7 15.7 %collective-permute-start.5 = (f32[32,16,128]{2,1,0:T(8,128)S(1)}, f32[32,16,128]{2,1,0:T(8,128)S(1)}, u32[]{:S(2)}, u32[]{:S(2)}) collective-permute-start(f32[32,16,128]{2,1,0:T(8,128)S(1)} %get-tuple-element.31), channel_id=1, source_target_pairs={{0,4},{4,8},{8,12},{12,16},{16,20},{20,24},{24,28},{28,32},{32,36}... | collective-permute-start | bytes 786440 | tf_op jit(solution)/shard_map/ppermute | solution.py:56
  17.8 43.0 %copy-start = (f32[64,4]{0,1:T(4,128)S(1)}, f32[64,4]{0,1:T(4,128)}, u32[]{:S(2)}) copy-start(f32[64,4]{0,1:T(4,128)} %param.15) | copy-start | bytes 3076
  21.5 2.1 %collective-permute-start.3 = (f32[32,8,128]{2,1,0:T(8,128)S(1)}, f32[32,8,128]{2,1,0:T(8,128)S(1)}, u32[]{:S(2)}, u32[]{:S(2)}) collective-permute-start(f32[32,8,128]{2,1,0:T(8,128)S(1)} %get-tuple-element.29), channel_id=1, source_target_pairs={{0,1},{1,0},{2,3},{3,2},{4,5},{5,4},{6,7},{7,6},{8,9},{9,8},{10,11... | collective-permute-start | bytes 393224 | tf_op jit(solution)/shard_map/ppermute | solution.py:60
  21.6 7.8 %collective-permute-start.4 = (f32[32,8,128]{2,1,0:T(8,128)S(1)}, f32[32,8,128]{2,1,0:T(8,128)S(1)}, u32[]{:S(2)}, u32[]{:S(2)}) collective-permute-start(f32[32,8,128]{2,1,0:T(8,128)S(1)} %get-tuple-element.30), channel_id=1, source_target_pairs={{1,2},{2,1},{5,6},{6,5},{9,10},{10,9},{13,14},{14,13},{17,18},{18,... | collective-permute-start | bytes 393224 | tf_op jit(solution)/shard_map/ppermute | solution.py:64
  62.4 16.6 %all-to-all-start.1 = ((f32[64,8,128]{2,1,0:T(8,128)}), f32[64,8,128]{2,1,0:T(8,128)S(1)}, u32[]{:S(2)}, u32[]{:S(2)}) async-start(f32[64,8,128]{2,1,0:T(8,128)} %get-tuple-element.32), calls=%async_computation.1 | async-start | bytes 524288 | tf_op jit(solution)/shard_map/all_to_all | solution.py:393
  67.2 1.2 %collective-permute-start.6 = (f32[1,128]{1,0:T(1,128)S(1)}, f32[1,128]{1,0:T(1,128)S(1)}, u32[]{:S(2)}, u32[]{:S(2)}) collective-permute-start(f32[1,128]{1,0:T(1,128)S(1)} %get-tuple-element.33), channel_id=1, source_target_pairs={{0,1},{1,0},{2,3},{3,2},{4,5},{5,4},{6,7},{7,6},{8,9},{9,8},{10,11... | collective-permute-start | bytes 1544 | tf_op jit(solution)/shard_map/ppermute | solution.py:60
  68.4 5.1 %collective-permute-start.7 = (f32[1,128]{1,0:T(1,128)S(1)}, f32[1,128]{1,0:T(1,128)S(1)}, u32[]{:S(2)}, u32[]{:S(2)}) collective-permute-start(f32[1,128]{1,0:T(1,128)S(1)} %add.6), channel_id=1, source_target_pairs={{0,2},{2,0},{1,3},{3,1},{4,6},{6,4},{5,7},{7,5},{8,10},{10,8},{9,1... | collective-permute-start | bytes 1544 | tf_op jit(solution)/shard_map/ppermute | solution.py:60

commit v4 on v3

--- a/solution.py
+++ b/solution.py
@@ -164,37 +164,48 @@
         copy.wait()
 
 
+def interior_kernel(checkpoint, advect, diffuse, history, coefs, initial):
+    lane = lane_index()
+    nothing = jnp.zeros((8, LANES), jnp.float32)
+    for g in range(GROUPS):
+        for tile in range(2):
+            rows = slice(OWN + 8 * tile, OWN + 8 * tile + 8)
+            values = coefficient_tiles(advect, diffuse, None, None, tile, g)
+            for which in range(5):
+                coefs[which, g, rows, :] = values[which]
+            for k in range(COMPS):
+                value = checkpoint[k, tile * 8 : tile * 8 + 8, lanes(g)]
+                initial[k * GROUPS + g, rows, :] = value
+        for k in range(COMPS):
+            initial[k * GROUPS + g, 0:8, :] = nothing
+            initial[k * GROUPS + g, TALL - 8 : TALL, :] = nothing
+    for moment in range(STEPS - 1):
+        first, tiles = (8, 2) if moment < 3 else (12, 1)
+        source = history.at[moment - 1] if moment else initial
+        stencil_step(source, history.at[moment], coefs, (0,) * 5, first, tiles, lane)
+
+
 def forward_kernel(
-    checkpoint, advect, diffuse, pair, other, obs_values,
-    history, last, observed, coefs, initial, arrival,
+    pair, other, obs_values, inner, inner_coefs, inner_initial,
+    history, coefs, initial, last, observed, arrival,
 ):
     fetch = pltpu.make_async_copy(obs_values, observed, arrival)
     fetch.start()
     lane = lane_index()
-    nothing = jnp.zeros((8, LANES), jnp.float32)
-    starts = (OWN, OWN + 8) + side_rows()
+    starts = side_rows()
     for g in range(GROUPS):
-        for tile in range(4):
-            rows = pl.ds(starts[tile], 8)
-            values = coefficient_tiles(advect, diffuse, pair, other, tile, g)
+        for tile in (2, 3):
+            rows = pl.ds(starts[tile - 2], 8)
+            values = coefficient_tiles(None, None, pair, other, tile, g)
             for which in range(5):
                 coefs[which, g, rows, :] = values[which]
             for k in range(COMPS):
-                if tile < 2:
-                    value = checkpoint[k, tile * 8 : tile * 8 + 8, lanes(g)]
-                else:
-                    value = (pair if tile == 2 else other)[8 * k : 8 * k + 8, lanes(g)]
+                value = (pair if tile == 2 else other)[8 * k : 8 * k + 8, lanes(g)]
                 initial[k * GROUPS + g, rows, :] = value
-        for k in range(COMPS):
-            initial[k * GROUPS + g, 0:8, :] = nothing
-            initial[k * GROUPS + g, TALL - 8 : TALL, :] = nothing
-
     for moment in range(STEPS):
-        first, tiles = ((0, 4), (4, 3), (8, 2))[(moment >= 3) + (moment >= 7)]
-        if tiles == 3:
-            first = moment + 1
         source = history.at[moment - 1] if moment else initial
-        stencil_step(source, history.at[moment], coefs, (0,) * 5, first, tiles, lane)
+        for first in (moment + 1, 23 - moment):
+            stencil_step(source, history.at[moment], coefs, (0,) * 5, first, 1, lane)
     for cell in range(CELLS):
         last[cell] = history[STEPS - 1, cell, OWN : OWN + 16, :]
     fetch.wait()
@@ -336,22 +347,28 @@
     pair = near(swapped(edge_pair, "space_1"))
     following = near(passed_along(start, TM, -1))
     weight = near(jnp.broadcast_to(obs_weight[None], (1, LANES)))
-    history, end_state, observed = pl.pallas_call(
+    sweep_shapes = (
+        local(STEPS, CELLS, TALL, LANES), local(5, GROUPS, TALL, LANES), local(CELLS, TALL, LANES)
+    )
+    inner = pl.pallas_call(
+        interior_kernel,
+        out_shape=sweep_shapes,
+        in_specs=[VMEM] * 3,
+        out_specs=(VMEM,) * 3,
+        name="interior",
+        compiler_params=GRANT,
+    )(initial, flow, spread)
+    history, _, _, end_state, observed = pl.pallas_call(
         forward_kernel,
-        out_shape=(
-            local(STEPS, CELLS, TALL, LANES), local(CELLS, ROWS, LANES),
-            local(STEPS, 2, COMPS, BLOCK, COLUMNS),
-        ),
-        in_specs=[VMEM] * 5 + [FAR],
-        out_specs=(VMEM,) * 3,
-        scratch_shapes=[
-            pltpu.VMEM((5, GROUPS, TALL, LANES), jnp.float32),
-            pltpu.VMEM((CELLS, TALL, LANES), jnp.float32),
-            pltpu.SemaphoreType.DMA(()),
-        ],
+        out_shape=sweep_shapes
+        + (local(CELLS, ROWS, LANES), local(STEPS, 2, COMPS, BLOCK, COLUMNS)),
+        in_specs=[VMEM, VMEM, FAR] + [VMEM] * 3,
+        out_specs=(VMEM,) * 5,
+        scratch_shapes=[pltpu.SemaphoreType.DMA(())],
+        input_output_aliases={3: 0, 4: 1, 5: 2},
         name="forward",
         compiler_params=GRANT,
-    )(initial, flow, spread, pair, other, far(obs_values[0]))
+    )(pair, other, far(obs_values[0]), *(near(value) for value in inner))
     prior_end = near(passed_along(end_state, TM, 1))
     own, to_pair, to_other = pl.pallas_call(
         adjoint_kernel,

time: 80.1 us -> 79 us (0.986)
  waiting for transfers between devices: 20.9 us -> 20 us
    ppermute x2, waiting for transfers between devices: 9.23 us -> 8.35 us  [crossed(): return lax.ppermute(value, SPACE, [(1, 2), (2, 1)])]
    pallas_call x1 -> x2, Pallas kernels: 2.64 us -> 2.46 us  [the longest x1 1.61 us: on_device(): pl.pallas_call(forward_kernel, out_shape=sweep_shapes + (local(CELLS, ROW...]
where the time goes in v4:
time: 79 us; the launch traced here: 78.6 us
  blocking collectives  31.2 us (39%)
  waiting for transfers between devices  20 us (25%)
  starting transfers between devices  15.9 us (20%)
  Pallas kernels  10.1 us (13%)
  between operations  1.43 us (2%)
    all_to_all x1, blocking collectives, on_device(): lax.all_to_all(parcels.reshape(windows, 1, 9 * LANES), TM, split_axis=0,...  31.2 us
    ppermute x2, waiting for transfers between devices, crossed(): return lax.ppermute(value, SPACE, [(1, 2), (2, 1)])  8.35 us
    ppermute x4, waiting for transfers between devices, swapped(): return lax.ppermute(value, axis, [(0, 1), (1, 0)])  6.22 us
    ppermute x2, starting transfers between devices, crossed(): return lax.ppermute(value, SPACE, [(1, 2), (2, 1)])  6.08 us
    all_to_all x1, waiting for transfers between devices, on_device(): lax.all_to_all(back, TM, split_axis=0, concat_axis=0, tiled=True)  5.46 us
    all_to_all x1, starting transfers between devices, on_device(): lax.all_to_all(back, TM, split_axis=0, concat_axis=0, tiled=True)  4.79 us
    ppermute x2, starting transfers between devices, passed_along(): lax.ppermute(value, axis, [(source, source + steps) for source in range(l...  4.7 us
    pallas_call x1, Pallas kernels, on_device(): pl.pallas_call(adjoint_kernel, out_shape=(local(CELLS, ROWS, LANES), loca...  3.6 us
  transfers between devices with their start and end apart: 9, of which 5 were waited for; matrix products, arithmetic and copies ran while one was open for 0% of the time, Pallas kernels for 8%

profile of v4, /device:TPU:16, one launch (start us, length us, event | category | flops | bytes accessed | tf_op | source)
XLA Modules:
  0.0 78.6 jit_solution(16356775248977684512)
XLA Ops:
  0.6 0.0 copy-start.1
  0.6 1.5 %edges.1 = (f32[56,1024]{1,0:T(8,128)S(1)}, f32[56,1024]{1,0:T(8,128)S(1)}, f32[5,16,1024]{2,1,0:T(8,128)S(1)}, f32[4,16,1024]{2,1,0:T(8,128)S(1)}, f32[2,16,102...) custom-call(f32[1,4]{1,0:T(1,128)} %inverse.1, f32[4,16,1024]{2,1,0:T(8,128)} %bitcast.20, ...), custom_call_target="tpu_custom_call" | custom-call | tf_op jit(solution)/shard_map/edges/pallas_call | solution.py:327
  2.2 0.1 collective-permute-start
  2.3 4.0 %collective-permute-start.1 = (f32[56,1024]{1,0:T(8,128)S(1)}, f32[56,1024]{1,0:T(8,128)S(1)}, u32[]{:S(2)}, u32[]{:S(2)}) collective-permute-start(f32[56,1024]{1,0:T(8,128)S(1)} %get-tuple-element.26), channel_id=1, source_target_pairs={{1,2},{2,1},{5,6},{6,5},{9,10},{10,9},{13,14},{14,13},{17,18},{18,... | collective-permute-start | bytes 688136 | tf_op jit(solution)/shard_map/ppermute | solution.py:64
  6.3 1.3 %collective-permute-start.2 = (f32[5,16,1024]{2,1,0:T(8,128)S(1)}, f32[5,16,1024]{2,1,0:T(8,128)S(1)}, u32[]{:S(2)}, u32[]{:S(2)}) collective-permute-start(f32[5,16,1024]{2,1,0:T(8,128)S(1)} %get-tuple-element.32), channel_id=1, source_target_pairs={{4,0},{8,4},{12,8},{16,12},{20,16},{24,20},{28,24},{32,28},{36,32}... | collective-permute-start | bytes 983048 | tf_op jit(solution)/shard_map/ppermute | solution.py:56
  7.6 0.9 %interior.1 = (f32[8,32,48,128]{3,2,1,0:T(8,128)S(1)}, f32[5,8,48,128]{3,2,1,0:T(8,128)S(1)}, f32[32,48,128]{2,1,0:T(8,128)S(1)}) custom-call(f32[4,16,1024]{2,1,0:T(8,128)S(1)} %get-tuple-element.27.checkpoint, f32[2,16,1024]{2,1,0:T(8,128)S(1)} %get-tuple-element.23.advect, f32[16,1024]{1,0:T(8,128)S(1)} %get-tuple-element.24.diffuse), custom_call_target="tpu_custom_call" | custom-call | tf_op jit(solution)/shard_map/interior/pallas_call | solution.py:353
  8.5 0.0 collective-permute-done.pair
  8.5 2.6 %collective-permute-done.1.other = f32[56,1024]{1,0:T(8,128)S(1)} collective-permute-done((f32[56,1024]{1,0:T(8,128)S(1)}, f32[56,1024]{1,0:T(8,128)S(1)}, u32[]{:S(2)}, u32[]{:S(2)}) %collective-permute-start.1) | collective-permute-done | bytes 229408 | tf_op jit(solution)/shard_map/ppermute | solution.py:64
  11.1 1.6 %forward.1 = (f32[8,32,48,128]{3,2,1,0:T(8,128)S(1)}, f32[5,8,48,128]{3,2,1,0:T(8,128)S(1)}, f32[32,48,128]{2,1,0:T(8,128)S(1)}, f32[32,16,128]{2,1,0:T(8,128)S(1)}, f32[8,2,4,8,1024]{4,3,2,1,0:T(8,128)S(1)}) custom-call(f32[56,1024]{1,0:T(8,128)S(1)} %collective-permute-done.pair, ...), custom_call_target="tpu_custom_call", output_to_operand_aliasing={{0}: (3, {}), {1}: (4, {}), {2}: (5, {})} | custom-call | tf_op jit(solution)/shard_map/forward/pallas_call | solution.py:361
  12.7 0.0 copy-start
  12.7 3.4 %collective-permute-start.5 = (f32[32,16,128]{2,1,0:T(8,128)S(1)}, f32[32,16,128]{2,1,0:T(8,128)S(1)}, u32[]{:S(2)}, u32[]{:S(2)}) collective-permute-start(f32[32,16,128]{2,1,0:T(8,128)S(1)} %get-tuple-element.37), channel_id=1, source_target_pairs={{0,4},{4,8},{8,12},{12,16},{16,20},{20,24},{24,28},{28,32},{32,36}... | collective-permute-start | bytes 786440 | tf_op jit(solution)/shard_map/ppermute | solution.py:56
  16.8 0.0 collective-permute-done.2.following
  16.8 0.0 copy-done.1
  16.8 3.6 %adjoint.1 = (f32[32,16,128]{2,1,0:T(8,128)S(1)}, f32[32,8,128]{2,1,0:T(8,128)S(1)}, f32[32,8,128]{2,1,0:T(8,128)S(1)}) custom-call(s32[2,8]{1,0:T(2,128)S(1)} %bitcast.18, f32[1,128]{1,0:T(1,128)S(1)} %broadcast_in_dim.12.weight, f32[2,16,1024]{2,1,0:T(8,128)S(1)} %get-tuple-element.23.advect, f32[16,1024]{1,0:T(8,128)S(1)} %get-tuple-element.24.diffuse, ...), custom_call_target="tpu_custom_call" | custom-call | tf_op jit(solution)/shard_map/adjoint/pallas_call | solution.py:373
  20.4 0.1 collective-permute-start.3
  20.5 2.0 %collective-permute-start.4 = (f32[32,8,128]{2,1,0:T(8,128)S(1)}, f32[32,8,128]{2,1,0:T(8,128)S(1)}, u32[]{:S(2)}, u32[]{:S(2)}) collective-permute-start(f32[32,8,128]{2,1,0:T(8,128)S(1)} %get-tuple-element.36), channel_id=1, source_target_pairs={{1,2},{2,1},{5,6},{6,5},{9,10},{10,9},{13,14},{14,13},{17,18},{18,... | collective-permute-start | bytes 393224 | tf_op jit(solution)/shard_map/ppermute | solution.py:64
  22.6 0.0 collective-permute-done.3.from_pair
  22.6 5.7 %collective-permute-done.4.from_other = f32[32,8,128]{2,1,0:T(8,128)S(1)} collective-permute-done((f32[32,8,128]{2,1,0:T(8,128)S(1)}, f32[32,8,128]{2,1,0:T(8,128)S(1)}, u32[]{:S(2)}, u32[]{:S(2)}) %collective-permute-start.4) | collective-permute-done | bytes 131104 | tf_op jit(solution)/shard_map/ppermute | solution.py:64
  28.3 0.0 collective-permute-done.5.prior_end
  28.3 0.1 gradient.1
  28.4 31.2 %all_to_all.10 = f32[64,1,1152]{2,1,0:T(1,128)S(1)} all-to-all(f32[64,1,1152]{2,1,0:T(1,128)S(1)} %bitcast.16), channel_id=1, replica_groups=mesh['tm_0'=8,'tm_1'=2,'tm_2'=4,'space_0'=2,'space_1'=2] {'tm_0','tm_1',..., dimensions={0} | all-to-all | bytes 589824 | tf_op jit(solution)/shard_map/all_to_all | solution.py:399
  59.7 0.0 copy-done
  59.7 1.6 %smoothing.1 = (f32[64,8,128]{2,1,0:T(8,128)}, f32[1,128]{1,0:T(1,128)S(1)}) custom-call(f32[4,64]{1,0:T(4,128)S(1)} %bitcast.17, f32[576,128]{1,0:T(8,128)S(1)} %bitcast.15), custom_call_target="tpu_custom_call" | custom-call | tf_op jit(solution)/shard_map/smoothing/pallas_call | solution.py:402
  61.2 4.8 %all-to-all-start.1 = ((f32[64,8,128]{2,1,0:T(8,128)}), f32[64,8,128]{2,1,0:T(8,128)S(1)}, u32[]{:S(2)}, u32[]{:S(2)}) async-start(f32[64,8,128]{2,1,0:T(8,128)} %get-tuple-element.38), calls=%async_computation.1 | async-start | bytes 524288 | tf_op jit(solution)/shard_map/all_to_all | solution.py:410
  66.0 0.1 collective-permute-start.6
  66.1 1.1 %collective-permute-done.6 = f32[1,128]{1,0:T(1,128)S(1)} collective-permute-done((f32[1,128]{1,0:T(1,128)S(1)}, f32[1,128]{1,0:T(1,128)S(1)}, u32[]{:S(2)}, u32[]{:S(2)}) %collective-permute-start.6) | collective-permute-done | bytes 544 | tf_op jit(solution)/shard_map/ppermute | solution.py:60
  67.3 0.0 collective-permute-start.7
  67.3 5.1 %collective-permute-done.7 = f32[1,128]{1,0:T(1,128)S(1)} collective-permute-done((f32[1,128]{1,0:T(1,128)S(1)}, f32[1,128]{1,0:T(1,128)S(1)}, u32[]{:S(2)}, u32[]{:S(2)}) %collective-permute-start.7) | collective-permute-done | bytes 544 | tf_op jit(solution)/shard_map/ppermute | solution.py:60
  72.4 5.5 %all-to-all-done.1.refs_0_ = f32[64,8,128]{2,1,0:T(8,128)S(1)} async-done(((f32[64,8,128]{2,1,0:T(8,128)}), f32[64,8,128]{2,1,0:T(8,128)S(1)}, u32[]{:S(2)}, u32[]{:S(2)}) %all-to-all-start.1) | async-done | bytes 262176 | tf_op jit(solution)/shard_map/all_to_all | solution.py:410
  77.8 0.8 %final.1 = (f32[4,16,1024]{2,1,0:T(8,128)}, f32[1,128]{1,0:T(1,128)}) custom-call(f32[64,8,128]{2,1,0:T(8,128)S(1)} %all-to-all-done.1.refs_0_, f32[1,128]{1,0:T(1,128)S(1)} %add.7.refs_1_), custom_call_target="tpu_custom_call" | custom-call | tf_op jit(solution)/shard_map/final/pallas_call | solution.py:414
  (3 shorter events, 0.0 us)
Async XLA Ops:
  0.6 16.2 %copy-start.1 = (s32[1,8,2]{1,2,0:T(2,128)S(1)}, s32[1,8,2]{1,2,0:T(2,128)}, u32[]{:S(2)}) copy-start(s32[1,8,2]{1,2,0:T(2,128)} %param.11) | copy-start | bytes 196
  2.2 6.3 %collective-permute-start = (f32[56,1024]{1,0:T(8,128)S(1)}, f32[56,1024]{1,0:T(8,128)S(1)}, u32[]{:S(2)}, u32[]{:S(2)}) collective-permute-start(f32[56,1024]{1,0:T(8,128)S(1)} %get-tuple-element.25), channel_id=1, source_target_pairs={{0,1},{1,0},{2,3},{3,2},{4,5},{5,4},{6,7},{7,6},{8,9},{9,8},{10,11... | collective-permute-start | bytes 688136 | tf_op jit(solution)/shard_map/ppermute | solution.py:60
  2.3 8.8 %collective-permute-start.1 = (f32[56,1024]{1,0:T(8,128)S(1)}, f32[56,1024]{1,0:T(8,128)S(1)}, u32[]{:S(2)}, u32[]{:S(2)}) collective-permute-start(f32[56,1024]{1,0:T(8,128)S(1)} %get-tuple-element.26), channel_id=1, source_target_pairs={{1,2},{2,1},{5,6},{6,5},{9,10},{10,9},{13,14},{14,13},{17,18},{18,... | collective-permute-start | bytes 688136 | tf_op jit(solution)/shard_map/ppermute | solution.py:64
  6.3 10.5 %collective-permute-start.2 = (f32[5,16,1024]{2,1,0:T(8,128)S(1)}, f32[5,16,1024]{2,1,0:T(8,128)S(1)}, u32[]{:S(2)}, u32[]{:S(2)}) collective-permute-start(f32[5,16,1024]{2,1,0:T(8,128)S(1)} %get-tuple-element.32), channel_id=1, source_target_pairs={{4,0},{8,4},{12,8},{16,12},{20,16},{24,20},{28,24},{32,28},{36,32}... | collective-permute-start | bytes 983048 | tf_op jit(solution)/shard_map/ppermute | solution.py:56
  12.7 47.0 %copy-start = (f32[64,4]{0,1:T(4,128)S(1)}, f32[64,4]{0,1:T(4,128)}, u32[]{:S(2)}) copy-start(f32[64,4]{0,1:T(4,128)} %param.15) | copy-start | bytes 3076
  12.7 15.6 %collective-permute-start.5 = (f32[32,16,128]{2,1,0:T(8,128)S(1)}, f32[32,16,128]{2,1,0:T(8,128)S(1)}, u32[]{:S(2)}, u32[]{:S(2)}) collective-permute-start(f32[32,16,128]{2,1,0:T(8,128)S(1)} %get-tuple-element.37), channel_id=1, source_target_pairs={{0,4},{4,8},{8,12},{12,16},{16,20},{20,24},{24,28},{28,32},{32,36}... | collective-permute-start | bytes 786440 | tf_op jit(solution)/shard_map/ppermute | solution.py:56
  20.4 2.2 %collective-permute-start.3 = (f32[32,8,128]{2,1,0:T(8,128)S(1)}, f32[32,8,128]{2,1,0:T(8,128)S(1)}, u32[]{:S(2)}, u32[]{:S(2)}) collective-permute-start(f32[32,8,128]{2,1,0:T(8,128)S(1)} %get-tuple-element.35), channel_id=1, source_target_pairs={{0,1},{1,0},{2,3},{3,2},{4,5},{5,4},{6,7},{7,6},{8,9},{9,8},{10,11... | collective-permute-start | bytes 393224 | tf_op jit(solution)/shard_map/ppermute | solution.py:60
  20.5 7.8 %collective-permute-start.4 = (f32[32,8,128]{2,1,0:T(8,128)S(1)}, f32[32,8,128]{2,1,0:T(8,128)S(1)}, u32[]{:S(2)}, u32[]{:S(2)}) collective-permute-start(f32[32,8,128]{2,1,0:T(8,128)S(1)} %get-tuple-element.36), channel_id=1, source_target_pairs={{1,2},{2,1},{5,6},{6,5},{9,10},{10,9},{13,14},{14,13},{17,18},{18,... | collective-permute-start | bytes 393224 | tf_op jit(solution)/shard_map/ppermute | solution.py:64
  61.2 16.6 %all-to-all-start.1 = ((f32[64,8,128]{2,1,0:T(8,128)}), f32[64,8,128]{2,1,0:T(8,128)S(1)}, u32[]{:S(2)}, u32[]{:S(2)}) async-start(f32[64,8,128]{2,1,0:T(8,128)} %get-tuple-element.38), calls=%async_computation.1 | async-start | bytes 524288 | tf_op jit(solution)/shard_map/all_to_all | solution.py:410
  66.0 1.2 %collective-permute-start.6 = (f32[1,128]{1,0:T(1,128)S(1)}, f32[1,128]{1,0:T(1,128)S(1)}, u32[]{:S(2)}, u32[]{:S(2)}) collective-permute-start(f32[1,128]{1,0:T(1,128)S(1)} %get-tuple-element.39), channel_id=1, source_target_pairs={{0,1},{1,0},{2,3},{3,2},{4,5},{5,4},{6,7},{7,6},{8,9},{9,8},{10,11... | collective-permute-start | bytes 1544 | tf_op jit(solution)/shard_map/ppermute | solution.py:60
  67.3 5.1 %collective-permute-start.7 = (f32[1,128]{1,0:T(1,128)S(1)}, f32[1,128]{1,0:T(1,128)S(1)}, u32[]{:S(2)}, u32[]{:S(2)}) collective-permute-start(f32[1,128]{1,0:T(1,128)S(1)} %add.6), channel_id=1, source_target_pairs={{0,2},{2,0},{1,3},{3,1},{4,6},{6,4},{5,7},{7,5},{8,10},{10,8},{9,1... | collective-permute-start | bytes 1544 | tf_op jit(solution)/shard_map/ppermute | solution.py:60
